TPU v7x, 256 devices: a whole 4x4x8 slice. The times are simulated.
256 devices in a mesh: io: 4 (over y_hi, core), comp: 64 (over y_lo, x, z).
Axes of the slice: x: 4, y: 4 (y_hi: 2, y_lo: 2; y = y_hi * 2 + y_lo), z: 8, core: 2. Of those that a mesh axis runs over, the one named last changes fastest.
Arguments:
- fields: float32 [786432, 256], P(('io', 'comp')), may hold values from -6 to 6
- file_offset: int32 [6144, 128], P(('io', 'comp')), may hold values from 0 to 786431, as said below
- level_remap: float32 [4, 64, 64], replicated, may hold values from -0.75 to 0.75
Outputs:
- history: float32 [786432, 256], P(('io', 'comp'))
Inputs may be any that keep to these rules, and one draw needn't show every extreme that they name: file_offset is a permutation of the 786432 file positions. The owner of a position p is the device of flat index p // 3072 (io index times the comp size plus comp index). A device's columns have as owners only itself, devices of its io index and devices of its comp index. To each other device of its io index it sends exactly 8 columns, except the two of comp index one above and one below (cyclically), which get 8 plus between 96 and 192; likewise along io with the devices of its comp index. Two neighbours exchange equally many columns each way, and the count 8 + 192 is reached in every draw. Which columns and positions is drawn.
All inputs are finite; a program needn't handle non-finite values.
Results may differ from a plain program's by a relative error of at most 0.00005.
Values sent between devices are 32-bit elements; how exact they have to be, the bound alone decides.
No kernel may reach another device: no remote copies, remote signals or barrier semaphores. Data moves between devices by JAX's collectives and lax.ppermute only.
A program may use at most 64 MiB of HBM per device.

v0:
```python
import jax
import jax.numpy as jnp
from jax import lax
from jax.sharding import PartitionSpec as P

SPREAD = 8
MOST = 192


def from_behind(value, axis, by):
    peers = lax.axis_size(axis)
    return lax.ppermute(value, axis, [(i, (i + by) % peers) for i in range(peers)])


def remap_levels(values, level_remap):
    field_count = level_remap.shape[0]
    levels = level_remap.shape[1]
    shaped = values.reshape(values.shape[0], field_count, levels)
    mixed = jnp.einsum("cfl,flm->cfm", shaped, level_remap, precision=lax.Precision.HIGHEST)
    return mixed.reshape(values.shape[0], field_count * levels)


def rank_within(target, active, count):
    length = target.shape[0]
    blocks = length // 128
    onehot = (
        (target[:, None] == jnp.arange(count, dtype=jnp.int32)[None, :]) & active[:, None]
    ).astype(jnp.float32)
    blocked = onehot.reshape(blocks, 128, count)
    lower = (jnp.arange(128)[:, None] > jnp.arange(128)[None, :]).astype(jnp.float32)
    inside = jnp.einsum("rs,bsk->brk", lower, blocked, precision=lax.Precision.HIGHEST)
    totals = jnp.sum(blocked, axis=1)
    earlier = (jnp.arange(blocks)[:, None] > jnp.arange(blocks)[None, :]).astype(jnp.float32)
    before = jnp.dot(earlier, totals, precision=lax.Precision.HIGHEST)
    counted = jnp.sum((inside + before[:, None, :]) * blocked, axis=2)
    return counted.reshape(length).astype(jnp.int32)


def pack_slots(values, offsets, slot_index, valid, slots):
    columns = values.shape[0]
    target = jnp.where(valid, slot_index, slots)
    source = (
        jnp.full((slots,), columns, jnp.int32)
        .at[target]
        .set(jnp.arange(columns, dtype=jnp.int32), mode="drop")
    )
    packed = jnp.take(values, source, axis=0, mode="fill", fill_value=0.0)
    packed_offsets = jnp.take(offsets, source, axis=0, mode="fill", fill_value=-1)
    return (packed, packed_offsets)


def per_device(fields, file_offset, level_remap):
    columns, width = fields.shape
    n_io = lax.axis_size("io")
    n_comp = lax.axis_size("comp")
    offsets = file_offset.reshape(columns)
    values = remap_levels(fields, level_remap)
    owner = offsets // columns
    my_group = lax.axis_index("io")
    my_task = lax.axis_index("comp")
    owner_group = owner // n_comp
    owner_task = owner % n_comp
    along_comp = (owner_group == my_group) & (owner_task != my_task)
    along_io = (owner_task == my_task) & (owner_group != my_group)
    stays = (owner_group == my_group) & (owner_task == my_task)
    comp_rank = rank_within(owner_task, along_comp, n_comp)
    io_rank = rank_within(owner_group, along_io, n_io)
    received = []
    comp_rows, comp_offsets = pack_slots(
        values,
        offsets,
        owner_task * SPREAD + comp_rank,
        along_comp & (comp_rank < SPREAD),
        n_comp * SPREAD,
    )
    got_rows, got_offsets = (
        lax.all_to_all(
            comp_rows.reshape(n_comp, SPREAD, width),
            "comp",
            split_axis=0,
            concat_axis=0,
            tiled=True,
        ),
        lax.all_to_all(
            comp_offsets.reshape(n_comp, SPREAD), "comp", split_axis=0, concat_axis=0, tiled=True
        ),
    )
    received.append(
        (got_rows.reshape(n_comp * SPREAD, width), got_offsets.reshape(n_comp * SPREAD))
    )
    io_rows, io_offsets = pack_slots(
        values,
        offsets,
        owner_group * SPREAD + io_rank,
        along_io & (io_rank < SPREAD),
        n_io * SPREAD,
    )
    got_rows, got_offsets = (
        lax.all_to_all(
            io_rows.reshape(n_io, SPREAD, width), "io", split_axis=0, concat_axis=0, tiled=True
        ),
        lax.all_to_all(
            io_offsets.reshape(n_io, SPREAD), "io", split_axis=0, concat_axis=0, tiled=True
        ),
    )
    received.append((got_rows.reshape(n_io * SPREAD, width), got_offsets.reshape(n_io * SPREAD)))
    extra_comp = along_comp & (comp_rank >= SPREAD)
    extra_io = along_io & (io_rank >= SPREAD)
    upper_rows, upper_offsets = pack_slots(
        values,
        offsets,
        comp_rank - SPREAD,
        extra_comp & (owner_task == (my_task + 1) % n_comp),
        MOST,
    )
    received.append(from_behind((upper_rows, upper_offsets), "comp", 1))
    lower_rows, lower_offsets = pack_slots(
        values,
        offsets,
        comp_rank - SPREAD,
        extra_comp & (owner_task == (my_task + n_comp - 1) % n_comp),
        MOST,
    )
    received.append(from_behind((lower_rows, lower_offsets), "comp", -1))
    upper_rows, upper_offsets = pack_slots(
        values, offsets, io_rank - SPREAD, extra_io & (owner_group == (my_group + 1) % n_io), MOST
    )
    received.append(from_behind((upper_rows, upper_offsets), "io", 1))
    lower_rows, lower_offsets = pack_slots(
        values,
        offsets,
        io_rank - SPREAD,
        extra_io & (owner_group == (my_group + n_io - 1) % n_io),
        MOST,
    )
    received.append(from_behind((lower_rows, lower_offsets), "io", -1))
    local_target = jnp.where(stays, offsets % columns, columns)
    all_rows = jnp.concatenate([values] + [pair[0] for pair in received], axis=0)
    all_targets = jnp.concatenate(
        [local_target]
        + [
            jnp.where(pair[1] >= 0, pair[1] % columns, columns).astype(jnp.int32)
            for pair in received
        ],
        axis=0,
    )
    total_rows = all_rows.shape[0]
    source = (
        jnp.zeros((columns,), jnp.int32)
        .at[all_targets]
        .set(jnp.arange(total_rows, dtype=jnp.int32), mode="drop")
    )
    placed = jnp.take(all_rows, source, axis=0)
    return placed


def solution(mesh):
    placed = (P(("io", "comp"), None), P(("io", "comp"), None), P())
    return jax.shard_map(
        per_device, mesh=mesh, in_specs=placed, out_specs=P(("io", "comp"), None), check_vma=False
    )
```

profile of v0, /device:TPU:1, one launch (start us, length us, event | category | flops | bytes accessed | tf_op | source)
XLA Modules:
  0.0 209.5 jit_solution(11869798752779266953)
XLA Ops:
  0.0 0.8 broadcast_divide_fusion
  0.8 0.7 compare_and_fusion.5
  3.2 11.8 %scatter_custom_fusion.1 = s32[32]{0:T(128)S(1)} fusion(s32[3072]{0:T(1024)S(1)} %bitcast.89, s32[3072]{0:T(1024)S(1)} %iota.64, s32[]{:T(128)} %constant.198.clone.1), kind=kCustom, calls=%fused_computation.167 | custom fusion | bytes 132 | tf_op jit(solution)/shard_map/scatter | solution.py:45
  15.0 11.8 %scatter_custom_fusion = s32[512]{0:T(512)S(1)} fusion(s32[3072]{0:T(1024)S(1)} %bitcast.88, s32[3072]{0:T(1024)S(1)} %iota.63, s32[]{:T(128)} %constant.198.clone.1), kind=kCustom, calls=%fused_computation.150 | custom fusion | bytes 2052 | tf_op jit(solution)/shard_map/scatter | solution.py:45
  26.8 1.4 gather_fusion.1
  29.4 6.4 %all-to-all-start.1 = ((s32[4,1,8]{2,1,0:T(1,128)}), s32[4,1,8]{2,1,0:T(1,128)S(1)}, u32[]{:S(2)}, u32[]{:S(2)}) async-start(s32[4,1,8]{2,1,0:T(1,128)} %bitcast.12), calls=%async_computation.1 | async-start | bytes 4096 | tf_op jit(solution)/shard_map/all_to_all | solution.py:102
  35.9 11.8 %scatter_custom_fusion.5 = s32[192]{0:T(256)S(1)} fusion(s32[3072]{0:T(1024)S(1)} %bitcast.86, s32[3072]{0:T(1024)S(1)} %iota.68, s32[]{:T(128)} %constant.198.clone.1), kind=kCustom, calls=%fused_computation.161 | custom fusion | bytes 772 | tf_op jit(solution)/shard_map/scatter | solution.py:45
  47.6 11.8 %scatter_custom_fusion.4 = s32[192]{0:T(256)S(1)} fusion(s32[3072]{0:T(1024)S(1)} %bitcast.87, s32[3072]{0:T(1024)S(1)} %iota.67, s32[]{:T(128)} %constant.198.clone.1), kind=kCustom, calls=%fused_computation.157 | custom fusion | bytes 772 | tf_op jit(solution)/shard_map/scatter | solution.py:45
  59.5 1.4 gather_fusion.7
  61.5 3.1 %collective-permute-start.2 = (s32[192]{0:T(256)}, s32[192]{0:T(256)}, u32[]{:S(2)}, u32[]{:S(2)}) collective-permute-start(s32[192]{0:T(256)} %get-tuple-element.9), channel_id=1, source_target_pairs={{0,64},{64,128},{128,192},{192,0},{1,65},{65,129},{129,193},{193,1... | collective-permute-start | bytes 2312 | tf_op jit(solution)/shard_map/ppermute | solution.py:12
  64.6 1.4 gather_fusion.8
  66.7 11.8 %scatter_custom_fusion.2 = s32[192]{0:T(256)S(1)} fusion(s32[3072]{0:T(1024)S(1)} %bitcast.85, s32[3072]{0:T(1024)S(1)} %iota.65, s32[]{:T(128)} %constant.198.clone.1), kind=kCustom, calls=%fused_computation.163 | custom fusion | bytes 772 | tf_op jit(solution)/shard_map/scatter | solution.py:45
  78.5 11.8 %scatter_custom_fusion.3 = s32[192]{0:T(256)S(1)} fusion(s32[3072]{0:T(1024)S(1)} %bitcast.84, s32[3072]{0:T(1024)S(1)} %iota.66, s32[]{:T(128)} %constant.198.clone.1), kind=kCustom, calls=%fused_computation.159 | custom fusion | bytes 772 | tf_op jit(solution)/shard_map/scatter | solution.py:45
  90.3 1.4 gather_fusion.5
  92.3 1.2 collective-permute-start
  93.5 1.4 gather_fusion.6
  95.5 6.3 %collective-permute-start.1 = (s32[192]{0:T(256)}, s32[192]{0:T(256)}, u32[]{:S(2)}, u32[]{:S(2)}) collective-permute-start(s32[192]{0:T(256)} %get-tuple-element.11), channel_id=1, source_target_pairs={{0,63},{1,0},{2,1},{3,2},{4,3},{5,4},{6,5},{7,6},{8,7},{9,8},{10,9... | collective-permute-start | bytes 2312 | tf_op jit(solution)/shard_map/ppermute | solution.py:12
  101.7 2.4 %copy.36 = f32[3072,256]{0,1:T(8,128)S(1)} copy(f32[3072,256]{1,0:T(8,128)} %param.7) | data formatting | bytes 6291456 | tf_op args[0]
  104.1 4.5 %fusion.47 = f32[4,64,3072]{2,1,0:T(8,128)} fusion(f32[4,64,64]{2,1,0:T(8,128)S(1)} %copy-done, f32[3072,4,64]{0,2,1:T(8,128)S(1)} %bitcast.78), kind=kOutput, calls=%fused_computation.169 | convolution fusion | flops 603979776 | bytes 6356992 | tf_op jit(solution)/shard_map/cfl,flm->cfm/dot_general | solution.py:19
  108.6 2.4 %copy.44 = f32[3072,256]{1,0:T(8,128)S(1)} copy(f32[3072,256]{0,1:T(8,128)} %bitcast.77) | data formatting | bytes 6291456 | tf_op jit(solution)/shard_map/reshape | solution.py:20
  111.0 0.9 gather_fusion.9
  111.9 0.8 broadcast_select_fusion.4
  112.7 0.7 gather_fusion.3
  113.4 1.5 gather_fusion.12
  115.0 1.5 gather_fusion.11
  116.5 0.9 gather_fusion.10
  117.4 3.1 %gather_fusion = s32[512]{0:T(512)S(1)} fusion(s32[3072]{0:T(1024)S(1)} %bitcast.76, s32[1024]{0:T(1024)S(1)} %get-tuple-element.39), kind=kCustom, calls=%fused_computation.8 | custom fusion | bytes 6144 | tf_op jit(solution)/shard_map/jit(_take)/gather | solution.py:48
  120.5 2.2 %gather_fusion.2 = f32[512,256]{1,0:T(8,128)} fusion(f32[3072,256]{1,0:T(8,128)S(1)} %copy.44, s32[1024]{0:T(1024)S(1)} %get-tuple-element.39), kind=kCustom, calls=%fused_computation.10 | custom fusion | bytes 1050624 | tf_op jit(solution)/shard_map/jit(_take)/gather | solution.py:47
  122.8 1.9 constant_dynamic-update-slice_fusion.4
  125.5 1.0 broadcast_select_fusion.1
  126.5 1.0 broadcast_select_fusion.2
  127.7 2.0 bitcast_select_fusion
  129.7 0.7 select_n.543
  130.4 8.0 %all-to-all-start = ((s32[64,1,8]{2,1,0:T(1,128)}), s32[64,1,8]{2,1,0:T(1,128)S(1)}, u32[]{:S(2)}, u32[]{:S(2)}) async-start(s32[64,1,8]{2,1,0:T(1,128)} %bitcast.7), calls=%async_computation | async-start | bytes 65536 | tf_op jit(solution)/shard_map/all_to_all | solution.py:84
  138.6 5.6 %collective-permute-start.5 = (f32[192,256]{1,0:T(8,128)S(1)}, f32[192,256]{1,0:T(8,128)S(1)}, u32[]{:S(2)}, u32[]{:S(2)}) collective-permute-start(f32[192,256]{1,0:T(8,128)S(1)} %broadcast_select_fusion.3), channel_id=1, source_target_pairs={{0,63},{1,0},{2,1},{3,2},{4,3},{5,4},{6,5},{7,6},{8,7},{9,8},{10,9... | collective-permute-start | bytes 589832 | tf_op jit(solution)/shard_map/ppermute | solution.py:12
  144.8 5.3 %collective-permute-start.6 = (f32[192,256]{1,0:T(8,128)S(1)}, f32[192,256]{1,0:T(8,128)S(1)}, u32[]{:S(2)}, u32[]{:S(2)}) collective-permute-start(f32[192,256]{1,0:T(8,128)S(1)} %broadcast_select_fusion.2), channel_id=1, source_target_pairs={{0,64},{64,128},{128,192},{192,0},{1,65},{65,129},{129,193},{193,1... | collective-permute-start | bytes 589832 | tf_op jit(solution)/shard_map/ppermute | solution.py:12
  151.6 5.1 %all-to-all-start.2 = ((f32[64,8,256]{2,1,0:T(8,128)}), f32[64,8,256]{2,1,0:T(8,128)S(1)}, u32[]{:S(2)}, u32[]{:S(2)}) async-start(f32[64,8,256]{2,1,0:T(8,128)} %bitcast_select_fusion), calls=%async_computation.2 | async-start | bytes 1048576 | tf_op jit(solution)/shard_map/all_to_all | solution.py:77
  156.7 0.7 compare_select_fusion.19
  158.1 21.7 %scatter_custom_fusion.6 = s32[3072]{0:T(1024)S(1)} fusion(s32[4384]{0:T(1024)S(1)} %fusion.17, s32[4384]{0:T(1024)S(1)} %iota.69, s32[]{:T(128)} %constant.196.clone.1), kind=kCustom, calls=%fused_computation.117 | custom fusion | bytes 12292 | tf_op jit(solution)/shard_map/scatter | solution.py:151
  179.9 5.8 %all-to-all-start.3 = ((f32[4,8,256]{2,1,0:T(8,128)}), f32[4,8,256]{2,1,0:T(8,128)S(1)}, u32[]{:S(2)}, u32[]{:S(2)}) async-start(f32[4,8,256]{2,1,0:T(8,128)} %bitcast_select_fusion.2), calls=%async_computation.3 | async-start | bytes 65536 | tf_op jit(solution)/shard_map/all_to_all | solution.py:99
  185.7 0.8 bitcast_dynamic-update-slice_fusion
  186.5 3.9 %all-to-all-done.3 = f32[4,8,256]{2,1,0:T(8,128)S(1)} async-done(((f32[4,8,256]{2,1,0:T(8,128)}), f32[4,8,256]{2,1,0:T(8,128)S(1)}, u32[]{:S(2)}, u32[]{:S(2)}) %all-to-all-start.3) | async-done | bytes 32800 | tf_op jit(solution)/shard_map/all_to_all | solution.py:99
  190.9 1.6 constant_dynamic-update-slice_fusion.3
  192.5 0.7 constant_dynamic-update-slice_fusion.2
  193.2 0.7 constant_dynamic-update-slice_fusion.1
  193.9 0.7 constant_dynamic-update-slice_fusion
  194.6 12.1 %gather_fusion.4 = f32[3072,256]{1,0:T(8,128)S(1)} fusion(f32[4384,256]{1,0:T(8,128)} %constant_dynamic-update-slice_fusion, s32[3072]{0:T(1024)S(1)} %fusion.28), kind=kCustom, calls=%fused_computation.12 | custom fusion | bytes 6303744 | tf_op jit(solution)/shard_map/jit(_take)/gather | solution.py:153
  206.7 2.7 %broadcast_select_fusion = f32[3072,256]{1,0:T(8,128)} fusion(f32[3072,256]{1,0:T(8,128)S(1)} %gather_fusion.4, pred[3072]{0:T(1024)(128)(4,1)S(1)} %compare_and_fusion.4), kind=kLoop, calls=%fused_computation.20 | loop fusion | flops 786432 | bytes 6294528 | tf_op jit(solution)/shard_map/jit(_take)/select_n | solution.py:153
  (85 shorter events, 9.7 us)
Async XLA Ops:
  0.0 104.1 %copy-start = (f32[4,64,64]{2,1,0:T(8,128)S(1)}, f32[4,64,64]{2,1,0:T(8,128)}, u32[]{:S(2)}) copy-start(f32[4,64,64]{2,1,0:T(8,128)} %param.9) | copy-start | bytes 196612
  0.0 59.4 %copy-start.1 = (s32[24,128]{1,0:T(8,128)S(1)}, s32[24,128]{1,0:T(8,128)}, u32[]{:S(2)}) copy-start(s32[24,128]{1,0:T(8,128)} %param.8) | copy-start | bytes 36868
  26.8 2.6 %copy-start.2 = (s32[1024]{0:T(1024)}, s32[1024]{0:T(1024)S(1)}, u32[]{:S(2)}) copy-start(s32[1024]{0:T(1024)S(1)} %get-tuple-element.38) | copy-start | bytes 12292
  29.4 100.9 %all-to-all-start.1 = ((s32[4,1,8]{2,1,0:T(1,128)}), s32[4,1,8]{2,1,0:T(1,128)S(1)}, u32[]{:S(2)}, u32[]{:S(2)}) async-start(s32[4,1,8]{2,1,0:T(1,128)} %bitcast.12), calls=%async_computation.1 | async-start | bytes 4096 | tf_op jit(solution)/shard_map/all_to_all | solution.py:102
  61.5 77.1 %collective-permute-start.2 = (s32[192]{0:T(256)}, s32[192]{0:T(256)}, u32[]{:S(2)}, u32[]{:S(2)}) collective-permute-start(s32[192]{0:T(256)} %get-tuple-element.9), channel_id=1, source_target_pairs={{0,64},{64,128},{128,192},{192,0},{1,65},{65,129},{129,193},{193,1... | collective-permute-start | bytes 2312 | tf_op jit(solution)/shard_map/ppermute | solution.py:12
  66.7 78.2 %collective-permute-start.3 = (s32[192]{0:T(256)}, s32[192]{0:T(256)}, u32[]{:S(2)}, u32[]{:S(2)}) collective-permute-start(s32[192]{0:T(256)} %get-tuple-element.6), channel_id=1, source_target_pairs={{0,192},{64,0},{128,64},{192,128},{1,193},{65,1},{129,65},{193,129... | collective-permute-start | bytes 2312 | tf_op jit(solution)/shard_map/ppermute | solution.py:12
  92.3 58.5 %collective-permute-start = (s32[192]{0:T(256)}, s32[192]{0:T(256)}, u32[]{:S(2)}, u32[]{:S(2)}) collective-permute-start(s32[192]{0:T(256)} %get-tuple-element.13), channel_id=1, source_target_pairs={{0,1},{1,2},{2,3},{3,4},{4,5},{5,6},{6,7},{7,8},{8,9},{9,10},{10,1... | collective-permute-start | bytes 2312 | tf_op jit(solution)/shard_map/ppermute | solution.py:12
  95.5 61.2 %collective-permute-start.1 = (s32[192]{0:T(256)}, s32[192]{0:T(256)}, u32[]{:S(2)}, u32[]{:S(2)}) collective-permute-start(s32[192]{0:T(256)} %get-tuple-element.11), channel_id=1, source_target_pairs={{0,63},{1,0},{2,1},{3,2},{4,3},{5,4},{6,5},{7,6},{8,7},{9,8},{10,9... | collective-permute-start | bytes 2312 | tf_op jit(solution)/shard_map/ppermute | solution.py:12
  112.7 78.3 %collective-permute-start.4 = (f32[192,256]{1,0:T(8,128)}, f32[192,256]{1,0:T(8,128)}, u32[]{:S(2)}, u32[]{:S(2)}) collective-permute-start(f32[192,256]{1,0:T(8,128)} %broadcast_select_fusion.4), channel_id=1, source_target_pairs={{0,1},{1,2},{2,3},{3,4},{4,5},{5,6},{6,7},{7,8},{8,9},{9,10},{10,1... | collective-permute-start | bytes 589832 | tf_op jit(solution)/shard_map/ppermute | solution.py:12
  122.8 1.9 copy-start.6
  122.8 2.8 %copy-start.4 = (pred[192]{0:T(512)(128)(4,1)S(1)}, pred[192]{0:T(512)(128)(4,1)}, u32[]{:S(2)}) copy-start(pred[192]{0:T(512)(128)(4,1)} %get-tuple-element.8) | copy-start | bytes 580
  122.8 3.8 %copy-start.3 = (pred[192]{0:T(512)(128)(4,1)S(1)}, pred[192]{0:T(512)(128)(4,1)}, u32[]{:S(2)}) copy-start(pred[192]{0:T(512)(128)(4,1)} %get-tuple-element.10) | copy-start | bytes 580
  122.8 4.8 %copy-start.5 = (pred[192]{0:T(512)(128)(4,1)S(1)}, pred[192]{0:T(512)(128)(4,1)}, u32[]{:S(2)}) copy-start(pred[192]{0:T(512)(128)(4,1)} %get-tuple-element.12) | copy-start | bytes 580
  130.4 21.2 %all-to-all-start = ((s32[64,1,8]{2,1,0:T(1,128)}), s32[64,1,8]{2,1,0:T(1,128)S(1)}, u32[]{:S(2)}, u32[]{:S(2)}) async-start(s32[64,1,8]{2,1,0:T(1,128)} %bitcast.7), calls=%async_computation | async-start | bytes 65536 | tf_op jit(solution)/shard_map/all_to_all | solution.py:84
  138.6 54.0 %collective-permute-start.5 = (f32[192,256]{1,0:T(8,128)S(1)}, f32[192,256]{1,0:T(8,128)S(1)}, u32[]{:S(2)}, u32[]{:S(2)}) collective-permute-start(f32[192,256]{1,0:T(8,128)S(1)} %broadcast_select_fusion.3), channel_id=1, source_target_pairs={{0,63},{1,0},{2,1},{3,2},{4,3},{5,4},{6,5},{7,6},{8,7},{9,8},{10,9... | collective-permute-start | bytes 589832 | tf_op jit(solution)/shard_map/ppermute | solution.py:12
  144.8 48.4 %collective-permute-start.6 = (f32[192,256]{1,0:T(8,128)S(1)}, f32[192,256]{1,0:T(8,128)S(1)}, u32[]{:S(2)}, u32[]{:S(2)}) collective-permute-start(f32[192,256]{1,0:T(8,128)S(1)} %broadcast_select_fusion.2), channel_id=1, source_target_pairs={{0,64},{64,128},{128,192},{192,0},{1,65},{65,129},{129,193},{193,1... | collective-permute-start | bytes 589832 | tf_op jit(solution)/shard_map/ppermute | solution.py:12
  150.8 43.1 %collective-permute-start.7 = (f32[192,256]{1,0:T(8,128)S(1)}, f32[192,256]{1,0:T(8,128)S(1)}, u32[]{:S(2)}, u32[]{:S(2)}) collective-permute-start(f32[192,256]{1,0:T(8,128)S(1)} %broadcast_select_fusion.1), channel_id=1, source_target_pairs={{0,192},{64,0},{128,64},{192,128},{1,193},{65,1},{129,65},{193,129... | collective-permute-start | bytes 589832 | tf_op jit(solution)/shard_map/ppermute | solution.py:12
  151.6 28.3 %all-to-all-start.2 = ((f32[64,8,256]{2,1,0:T(8,128)}), f32[64,8,256]{2,1,0:T(8,128)S(1)}, u32[]{:S(2)}, u32[]{:S(2)}) async-start(f32[64,8,256]{2,1,0:T(8,128)} %bitcast_select_fusion), calls=%async_computation.2 | async-start | bytes 1048576 | tf_op jit(solution)/shard_map/all_to_all | solution.py:77
  179.9 10.5 %all-to-all-start.3 = ((f32[4,8,256]{2,1,0:T(8,128)}), f32[4,8,256]{2,1,0:T(8,128)S(1)}, u32[]{:S(2)}, u32[]{:S(2)}) async-start(f32[4,8,256]{2,1,0:T(8,128)} %bitcast_select_fusion.2), calls=%async_computation.3 | async-start | bytes 65536 | tf_op jit(solution)/shard_map/all_to_all | solution.py:99
where the time goes:
time: 210 us; the launch traced here: 209 us
  local copies, waits for them, and re-layouts  136 us (65%)
  starting transfers between devices  46.9 us (22%)
  other arithmetic  16.5 us (8%)
  matrix products  5.35 us (3%)
  waiting for transfers between devices  3.88 us (2%)
    scatter x6, local copies, waits for them, and re-layouts, pack_slots(): source = jnp.full((slots,), columns, jnp.int32).at[target].set(jnp.arange...  70.6 us
    scatter x1, local copies, waits for them, and re-layouts, per_device(): source = jnp.zeros((columns,), jnp.int32).at[all_targets].set(jnp.arange(...  21.7 us
    ppermute x8, starting transfers between devices, from_behind(): lax.ppermute(value, axis, [(i, (i + by) % peers) for i in range(peers)])  21.6 us
    gather x1, local copies, waits for them, and re-layouts, per_device(): placed = jnp.take(all_rows, source, axis=0)  12.1 us
    gather x6, local copies, waits for them, and re-layouts, pack_slots(): jnp.take(offsets, source, axis=0, mode='fill', fill_value=-1)  10.3 us
    unnamed x21, local copies, waits for them, and re-layouts  8.68 us
    all_to_all x1, starting transfers between devices, per_device(): lax.all_to_all(comp_offsets.reshape(n_comp, SPREAD), 'comp', split_axis=0...  7.97 us
    gather x6, local copies, waits for them, and re-layouts, pack_slots(): packed = jnp.take(values, source, axis=0, mode='fill', fill_value=0.0)  7.77 us
  transfers between devices with their start and end apart: 12, of which 1 were waited for; matrix products, arithmetic and copies ran while one was open for 54% of the time, Pallas kernels for 0%

commit v1 on v0

v1 whole, which is shorter than its diff:
```python
import jax
import jax.numpy as jnp
from jax import lax
from jax.experimental import pallas as pl
from jax.experimental.pallas import tpu as pltpu
from jax.sharding import PartitionSpec as P

SPREAD = 8
MOST = 192
COLUMNS = 3072
BLOCKS = COLUMNS // 128
WIDTH = 256
N_COMP = 64
N_IO = 4
PACKET = 2 * SPREAD + 1
NEAR_COMP = MOST
NEAR_IO = MOST + SPREAD
COMP_ROWS = 392
IO_ROWS = 408
FAR_ROWS = 24
KEYS = 80
DUMP = COLUMNS
PLACED = 2 * (COLUMNS + 8)
VMEM = pltpu.VMEM
SMEM = pltpu.SMEM


def coordinates():
    return lax.axis_index("io"), lax.axis_index("comp")


def pack_kernel(
    offsets_ref,
    fields_ref,
    spread_ref,
    up_ref,
    down_ref,
    next_ref,
    prev_ref,
    far_ref,
    stay_ref,
    fields,
    onehot,
    prefix,
    ranks,
    high,
    low,
    source,
    source_s,
    sems,
):
    fetch = pltpu.make_async_copy(fields_ref, fields, sems.at[0])
    fetch.start()
    group, task = coordinates()
    offset = offsets_ref[...]
    owner = ((offset >> 10) * 21846) >> 16
    position = offset - owner * COLUMNS
    owner_group = owner >> 6
    owner_task = owner & (N_COMP - 1)
    along_comp = (owner_group == group) & (owner_task != task)
    along_io = (owner_task == task) & (owner_group != group)
    key = jnp.where(along_comp, owner_task, jnp.where(along_io, N_COMP + owner_group, 127))
    rows = lax.broadcasted_iota(jnp.int32, (KEYS, 128), 0)
    for b in range(BLOCKS):
        hit = rows == key[b : b + 1, :]
        onehot[b * KEYS : (b + 1) * KEYS, :] = jnp.where(hit, 1.0, 0.0).astype(jnp.bfloat16)
    r = lax.broadcasted_iota(jnp.int32, (128, 256), 0)
    c = lax.broadcasted_iota(jnp.int32, (128, 256), 1)
    earlier = jnp.where((r < c) | (c >= 128), 1.0, 0.0).astype(jnp.bfloat16)
    prefix[...] = jnp.dot(onehot[...], earlier, preferred_element_type=jnp.float32)
    carry = jnp.zeros((KEYS, 128), jnp.float32)
    for b in range(BLOCKS):
        hit = rows == key[b : b + 1, :]
        counted = prefix[b * KEYS : (b + 1) * KEYS, 0:128] + carry
        ranks[b : b + 1, :] = jnp.sum(jnp.where(hit, counted, 0.0), axis=0, keepdims=True)
        carry = carry + prefix[b * KEYS : (b + 1) * KEYS, 128:256]
    rank = ranks[...].astype(jnp.int32)
    upper = (task + 1) & (N_COMP - 1)
    after = (group + 1) & (N_IO - 1)
    before = (group + N_IO - 1) & (N_IO - 1)
    comp_slot = jnp.where(
        rank < SPREAD,
        owner_task * SPREAD + rank,
        jnp.where(owner_task == upper, 512, 768) + rank - SPREAD,
    )
    io_slot = (
        jnp.where(owner_group == after, 1024, jnp.where(owner_group == before, 1280, 1536)) + rank
    )
    slot = jnp.where(along_comp, comp_slot, jnp.where(along_io, io_slot, 2047))
    stay_ref[...] = jnp.where(along_comp | along_io, DUMP, position)
    slot_high = slot >> 7
    slot_low = slot & 127
    column = lax.broadcasted_iota(jnp.int32, (BLOCKS, 128), 0) * 128 + lax.broadcasted_iota(
        jnp.int32, (BLOCKS, 128), 1
    )
    coded = position + 1
    parts = [
        (column & 255).astype(jnp.float32),
        (column >> 8).astype(jnp.float32),
        (coded & 255).astype(jnp.float32),
        (coded >> 8).astype(jnp.float32),
    ]
    rows16 = lax.broadcasted_iota(jnp.int32, (16, 128), 0)
    rows128 = lax.broadcasted_iota(jnp.int32, (128, 128), 0)
    for b in range(BLOCKS):
        hit = rows16 == slot_high[b : b + 1, :]
        for j in range(4):
            high[16 * j : 16 * (j + 1), 128 * b : 128 * (b + 1)] = jnp.where(
                hit, parts[j][b : b + 1, :], 0.0
            ).astype(jnp.bfloat16)
        low[:, 128 * b : 128 * (b + 1)] = jnp.where(
            rows128 == slot_low[b : b + 1, :], 1.0, 0.0
        ).astype(jnp.bfloat16)
    found = lax.dot_general(
        high[...], low[...], (((1,), (1,)), ((), ())), preferred_element_type=jnp.float32
    )
    chosen = (found[0:16, :] + 256.0 * found[16:32, :]).astype(jnp.int32)
    source[...] = (chosen >> 3) * 16 + (chosen & 7)
    push = pltpu.make_async_copy(source, source_s, sems.at[1])
    push.start()
    coded = found[32:48, :] + 256.0 * found[48:64, :]
    goal = jnp.where(coded > 0.5, coded - 1.0, float(DUMP))
    for t in range(N_COMP):
        spread_ref[PACKET * t + 2 * SPREAD : PACKET * (t + 1), :] = goal[t >> 4 : (t >> 4) + 1, :]
    up_ref[0:2, :] = goal[4:6, :]
    down_ref[0:2, :] = goal[6:8, :]
    next_ref[0:2, :] = goal[8:10, :]
    prev_ref[0:2, :] = goal[10:12, :]
    far_ref[0:1, :] = goal[12:13, :]
    push.wait()
    fetch.wait()

    def copy(into, at, row):
        into[pl.ds(at, 1), :] = fields[pl.ds(row, 1), :]
        into[pl.ds(at + 1, 1), :] = fields[pl.ds(row + 8, 1), :]

    def spread_step(i, _):
        for k in range(32):
            copy(spread_ref, i * (4 * PACKET) + (k // 8) * PACKET + 2 * (k % 8), source_s[i // 4, (i % 4) * 32 + k])
        return 0

    lax.fori_loop(0, 16, spread_step, 0)

    def near_step(into, base):
        def step(i, _):
            for k in range(8):
                copy(into, 2 + 16 * i + 2 * k, source_s[base + i // 16, (i % 16) * 8 + k])
            return 0

        return step

    lax.fori_loop(0, NEAR_COMP // 8, near_step(up_ref, 4), 0)
    lax.fori_loop(0, NEAR_COMP // 8, near_step(down_ref, 6), 0)
    lax.fori_loop(0, NEAR_IO // 8, near_step(next_ref, 8), 0)
    lax.fori_loop(0, NEAR_IO // 8, near_step(prev_ref, 10), 0)
    for k in range(SPREAD):
        copy(far_ref, 1 + 2 * k, source_s[12, k])


def local_kernel(stay_ref, fields_ref, remap_ref, placed_ref, high_ref, low_ref):
    zero = jnp.zeros((64, 64), jnp.float32)
    for f in range(4):
        band = jnp.concatenate([remap_ref[f] if g == f else zero for g in range(4)], axis=1)
        top = band.astype(jnp.bfloat16)
        high_ref[64 * f : 64 * (f + 1), :] = top
        low_ref[64 * f : 64 * (f + 1), :] = (band - top.astype(jnp.float32)).astype(jnp.bfloat16)

    def step(i, _):
        for k in range(16):
            at = 2 * stay_ref[i // 8, (i % 8) * 16 + k]
            row = 32 * i + 16 * (k // 8) + k % 8
            placed_ref[pl.ds(at, 1), :] = fields_ref[pl.ds(row, 1), :]
            placed_ref[pl.ds(at + 1, 1), :] = fields_ref[pl.ds(row + 8, 1), :]
        return 0

    lax.fori_loop(0, COLUMNS // 16, step, 0)


def final_kernel(
    spread_ref,
    up_ref,
    down_ref,
    next_ref,
    prev_ref,
    far_ref,
    placed_in,
    high_ref,
    low_ref,
    out_ref,
    placed,
    goal,
    goal_s,
    result,
    sems,
):
    fetch = pltpu.make_async_copy(placed_in, placed, sems.at[1])
    fetch.start()
    _, task = coordinates()
    for t in range(N_COMP):
        goal[t : t + 1, :] = spread_ref[PACKET * t + 2 * SPREAD : PACKET * (t + 1), :].astype(jnp.int32)
    for j, ref in enumerate((up_ref, down_ref, next_ref, prev_ref)):
        goal[64 + 2 * j : 66 + 2 * j, :] = ref[0:2, :].astype(jnp.int32)
    goal[72:73, :] = far_ref[0:1, :].astype(jnp.int32)
    push = pltpu.make_async_copy(goal, goal_s, sems.at[0])
    push.start()
    push.wait()
    fetch.wait()

    def copy(origin, at, row):
        to = 2 * row
        placed[pl.ds(to, 1), :] = origin[pl.ds(at, 1), :]
        placed[pl.ds(to + 1, 1), :] = origin[pl.ds(at + 1, 1), :]

    lane = (task & 15) * SPREAD

    def spread_step(i, _):
        for k in range(16):
            copy(spread_ref, i * (2 * PACKET) + (k // 8) * PACKET + 2 * (k % 8), goal_s[2 * i + k // 8, lane + k % 8])
        return 0

    lax.fori_loop(0, 32, spread_step, 0)

    def near_step(origin, base):
        def step(i, _):
            for k in range(8):
                copy(origin, 2 + 16 * i + 2 * k, goal_s[base + i // 16, (i % 16) * 8 + k])
            return 0

        return step

    lax.fori_loop(0, NEAR_COMP // 8, near_step(up_ref, 64), 0)
    lax.fori_loop(0, NEAR_COMP // 8, near_step(down_ref, 66), 0)
    lax.fori_loop(0, NEAR_IO // 8, near_step(next_ref, 68), 0)
    lax.fori_loop(0, NEAR_IO // 8, near_step(prev_ref, 70), 0)
    for k in range(SPREAD):
        copy(far_ref, 1 + 2 * k, goal_s[72, k])

    size = 512
    copies = []
    for j in range(COLUMNS // size):
        left = placed[pl.ds(2 * size * j, size, stride=2), :]
        right = placed[pl.ds(2 * size * j + 1, size, stride=2), :]
        x = jnp.concatenate([left, right], axis=1)
        x_high = x.astype(jnp.bfloat16)
        x_low = (x - x_high.astype(jnp.float32)).astype(jnp.bfloat16)
        total = jnp.dot(x_high, high_ref[...], preferred_element_type=jnp.float32)
        total += jnp.dot(x_high, low_ref[...], preferred_element_type=jnp.float32)
        total += jnp.dot(x_low, high_ref[...], preferred_element_type=jnp.float32)
        result[size * j : size * (j + 1), :] = total
        write = pltpu.make_async_copy(
            result.at[pl.ds(size * j, size), :],
            out_ref.at[pl.ds(size * j, size), :],
            sems.at[2 + j],
        )
        write.start()
        copies.append(write)
    for write in copies:
        write.wait()


def shift(value, axis, by):
    peers = lax.axis_size(axis)
    return lax.ppermute(value, axis, [(i, (i + by) % peers) for i in range(peers)])


def per_device(fields, file_offset, level_remap):
    f32 = jnp.float32
    whole = pl.BlockSpec(memory_space=VMEM)
    anywhere = pl.BlockSpec(memory_space=pl.ANY)
    scalars = pl.BlockSpec(memory_space=SMEM)
    fields = (
        fields.reshape(COLUMNS // 8, 8, 2, 128).transpose(0, 2, 1, 3).reshape(2 * COLUMNS, 128)
    )
    spread, up, down, after, before, far, stay = pl.pallas_call(
        pack_kernel,
        name="pack",
        out_shape=[
            jax.ShapeDtypeStruct((N_COMP * PACKET, 128), f32),
            jax.ShapeDtypeStruct((COMP_ROWS, 128), f32),
            jax.ShapeDtypeStruct((COMP_ROWS, 128), f32),
            jax.ShapeDtypeStruct((IO_ROWS, 128), f32),
            jax.ShapeDtypeStruct((IO_ROWS, 128), f32),
            jax.ShapeDtypeStruct((FAR_ROWS, 128), f32),
            jax.ShapeDtypeStruct((BLOCKS, 128), jnp.int32),
        ],
        in_specs=[whole, anywhere],
        out_specs=[whole] * 7,
        scratch_shapes=[
            VMEM((2 * COLUMNS, 128), f32),
            VMEM((BLOCKS * KEYS, 128), jnp.bfloat16),
            VMEM((BLOCKS * KEYS, 256), f32),
            VMEM((BLOCKS, 128), f32),
            VMEM((64, COLUMNS), jnp.bfloat16),
            VMEM((128, COLUMNS), jnp.bfloat16),
            VMEM((16, 128), jnp.int32),
            SMEM((16, 128), jnp.int32),
            pltpu.SemaphoreType.DMA((2,)),
        ],
        cost_estimate=pl.CostEstimate(flops=20_000_000, bytes_accessed=5_000_000, transcendentals=0),
    )(file_offset, fields)
    spread = lax.all_to_all(
        spread.reshape(N_COMP, 1, PACKET * 128), "comp", split_axis=0, concat_axis=0, tiled=True
    ).reshape(N_COMP * PACKET, 128)
    up = shift(up, "comp", 1)
    down = shift(down, "comp", -1)
    after = shift(after, "io", 1)
    before = shift(before, "io", -1)
    far = shift(far, "io", 2)
    placed, high, low = pl.pallas_call(
        local_kernel,
        name="local",
        out_shape=[
            jax.ShapeDtypeStruct((PLACED, 128), f32),
            jax.ShapeDtypeStruct((WIDTH, WIDTH), jnp.bfloat16),
            jax.ShapeDtypeStruct((WIDTH, WIDTH), jnp.bfloat16),
        ],
        in_specs=[scalars, whole, whole],
        out_specs=[whole] * 3,
        cost_estimate=pl.CostEstimate(flops=4_000_000_000, bytes_accessed=6_000_000, transcendentals=0),
    )(stay, fields, level_remap)
    return pl.pallas_call(
        final_kernel,
        name="final",
        out_shape=jax.ShapeDtypeStruct((COLUMNS, WIDTH), f32),
        in_specs=[whole] * 6 + [anywhere, whole, whole],
        out_specs=anywhere,
        scratch_shapes=[
            VMEM((PLACED, 128), f32),
            VMEM((80, 128), jnp.int32),
            SMEM((80, 128), jnp.int32),
            VMEM((COLUMNS, WIDTH), f32),
            pltpu.SemaphoreType.DMA((2 + COLUMNS // 512,)),
        ],
        cost_estimate=pl.CostEstimate(flops=1_000_000_000, bytes_accessed=8_000_000, transcendentals=0),
    )(spread, up, down, after, before, far, placed, high, low)


def solution(mesh):
    placed = (P(("io", "comp"), None), P(("io", "comp"), None), P())
    return jax.shard_map(
        per_device, mesh=mesh, in_specs=placed, out_specs=P(("io", "comp"), None), check_vma=False
    )
```

time: 210 us -> 57.6 us (0.27)
  local copies, waits for them, and re-layouts: 136 us -> 0.86 us
  Pallas kernels: 0 us -> 30.7 us
  starting transfers between devices: 46.9 us -> 24.4 us
  other arithmetic: 16.5 us -> 0 us
  matrix products: 5.35 us -> 0 us
  waiting for transfers between devices: 3.88 us -> 1.2 us
    scatter x7 -> x0, local copies, waits for them, and re-layouts: 92.3 us -> none  [the longest x6 70.6 us: pack_slots(): source = jnp.full((slots,), columns, jnp.int32).at[target].set(jnp.arange...]
    pallas_call x0 -> x3, Pallas kernels: none -> 30.7 us  [the longest x1 13 us: per_device(): pl.pallas_call(local_kernel, name='local', out_shape=[jax.ShapeDtypeStruc...]
    gather x13 -> x0, local copies, waits for them, and re-layouts: 30.2 us -> none  [the longest x1 12.1 us: per_device(): placed = jnp.take(all_rows, source, axis=0)]
    select_n x28 -> x0, other arithmetic: 14.2 us -> none  [the longest x6 5.54 us: pack_slots(): packed = jnp.take(values, source, axis=0, mode='fill', fill_value=0.0)]
    all_to_all x4 -> x1, starting transfers between devices: 25.3 us -> 13.5 us  [per_device(): lax.all_to_all(spread.reshape(N_COMP, 1, PACKET * 128), 'comp', split_axi...]
    ppermute x8 -> x5, starting transfers between devices: 21.6 us -> 10.9 us  [shift(): lax.ppermute(value, axis, [(i, (i + by) % peers) for i in range(peers)])]
    unnamed x21 -> x12, local copies, waits for them, and re-layouts: 8.68 us -> 0.86 us
    dot_general x5 -> x0, matrix products: 5.35 us -> none  [the longest x1 4.51 us: remap_levels(): jnp.einsum('cfl,flm->cfm', shaped, level_remap, precision=lax.Precision.H...]
  transfers between devices with their start and end apart: 12 -> 6, of which waited for: 1 -> 1; matrix products, arithmetic and copies ran while one was open for 54% -> 0% of each run, Pallas kernels for 0% -> 23%
where the time goes in v1:
time: 57.6 us; the launch traced here: 57.2 us
  Pallas kernels  30.7 us (53%)
  starting transfers between devices  24.4 us (42%)
  waiting for transfers between devices  1.2 us (2%)
  local copies, waits for them, and re-layouts  0.86 us (1%)
    all_to_all x1, starting transfers between devices, per_device(): lax.all_to_all(spread.reshape(N_COMP, 1, PACKET * 128), 'comp', split_axi...  13.5 us
    pallas_call x1, Pallas kernels, per_device(): pl.pallas_call(local_kernel, name='local', out_shape=[jax.ShapeDtypeStruc...  13 us
    ppermute x5, starting transfers between devices, shift(): lax.ppermute(value, axis, [(i, (i + by) % peers) for i in range(peers)])  10.9 us
    pallas_call x1, Pallas kernels, per_device(): pl.pallas_call(final_kernel, name='final', out_shape=jax.ShapeDtypeStruct...  10.1 us
    pallas_call x1, Pallas kernels, per_device(): pl.pallas_call(pack_kernel, name='pack', out_shape=[jax.ShapeDtypeStruct(...  7.62 us
    ppermute x5, waiting for transfers between devices, shift(): lax.ppermute(value, axis, [(i, (i + by) % peers) for i in range(peers)])  1.19 us
  transfers between devices with their start and end apart: 6, of which 1 were waited for; matrix products, arithmetic and copies ran while one was open for 0% of the time, Pallas kernels for 23%

profile of v1, /device:TPU:1, one launch (start us, length us, event | category | flops | bytes accessed | tf_op | source)
XLA Modules:
  0.0 57.2 jit_solution(5420550496770261234)
XLA Ops:
  0.0 7.6 %pack.1 = (f32[1088,128]{1,0:T(8,128)}, f32[392,128]{1,0:T(8,128)}, f32[392,128]{1,0:T(8,128)}, f32[408,128]{1,0:T(8,128)}, f32[408,128]{1,0:T(8,128)}, /*index=5*/f32[24,128]{1,0:T(8,128)}, s32[24,128]{1,0:T(8,128)}) custom-call(s32[24,128]{1,0:T(8,128)} %offsets_ref.1, f32[6144,128]{1,0:T(8,128)} %bitcast.7), custom_call_target="tpu_custom_call" | custom-call | flops 20000000 | bytes 5000000 | tf_op jit(solution)/shard_map/pack/pallas_call | solution.py:274
  7.6 13.5 %all-to-all-start = ((f32[64,1,2176]{2,1,0:T(1,128)}), f32[64,1,2176]{2,1,0:T(1,128)S(1)}, u32[]{:S(2)}, u32[]{:S(2)}) async-start(f32[64,1,2176]{2,1,0:T(1,128)} %bitcast.10), calls=%async_computation | async-start | bytes 1114112 | tf_op jit(solution)/shard_map/all_to_all | solution.py:301
  21.1 2.7 %collective-permute-start.4 = (f32[24,128]{1,0:T(8,128)}, f32[24,128]{1,0:T(8,128)S(1)}, u32[]{:S(2)}, u32[]{:S(2)}) collective-permute-start(f32[24,128]{1,0:T(8,128)} %get-tuple-element.20), channel_id=1, source_target_pairs={{0,128},{64,192},{128,0},{192,64},{1,129},{65,193},{129,1},{193,65... | collective-permute-start | bytes 36872 | tf_op jit(solution)/shard_map/ppermute | solution.py:263
  23.8 1.0 %collective-permute-start = (f32[392,128]{1,0:T(8,128)}, f32[392,128]{1,0:T(8,128)S(1)}, u32[]{:S(2)}, u32[]{:S(2)}) collective-permute-start(f32[392,128]{1,0:T(8,128)} %get-tuple-element.16), channel_id=1, source_target_pairs={{0,1},{1,2},{2,3},{3,4},{4,5},{5,6},{6,7},{7,8},{8,9},{9,10},{10,1... | collective-permute-start | bytes 602120 | tf_op jit(solution)/shard_map/ppermute | solution.py:263
  24.9 4.7 %collective-permute-start.1 = (f32[392,128]{1,0:T(8,128)}, f32[392,128]{1,0:T(8,128)S(1)}, u32[]{:S(2)}, u32[]{:S(2)}) collective-permute-start(f32[392,128]{1,0:T(8,128)} %get-tuple-element.17), channel_id=1, source_target_pairs={{0,63},{1,0},{2,1},{3,2},{4,3},{5,4},{6,5},{7,6},{8,7},{9,8},{10,9... | collective-permute-start | bytes 602120 | tf_op jit(solution)/shard_map/ppermute | solution.py:263
  29.5 2.5 %collective-permute-start.2 = (f32[408,128]{1,0:T(8,128)}, f32[408,128]{1,0:T(8,128)S(1)}, u32[]{:S(2)}, u32[]{:S(2)}) collective-permute-start(f32[408,128]{1,0:T(8,128)} %get-tuple-element.18), channel_id=1, source_target_pairs={{0,64},{64,128},{128,192},{192,0},{1,65},{65,129},{129,193},{193,1... | collective-permute-start | bytes 626696 | tf_op jit(solution)/shard_map/ppermute | solution.py:263
  32.0 0.0 collective-permute-start.3
  32.0 13.0 %local.1 = (f32[6160,128]{1,0:T(8,128)}, bf16[256,256]{1,0:T(8,128)(2,1)}, bf16[256,256]{1,0:T(8,128)(2,1)}) custom-call(s32[24,128]{1,0:T(8,128)} %get-tuple-element.21.stay_ref, f32[6144,128]{1,0:T(8,128)} %bitcast.8, f32[4,64,64]{2,1,0:T(8,128)} %remap_ref.1), custom_call_target="tpu_custom_call" | custom-call | flops 4000000000 | bytes 6000000 | tf_op jit(solution)/shard_map/local/pallas_call | solution.py:309
  45.0 0.0 collective-permute-done.4.far_ref
  45.0 0.0 copy-start.5
  45.0 0.0 collective-permute-done.up_ref
  45.0 0.0 copy-start.3
  45.1 0.0 collective-permute-done.1.down_ref
  45.1 0.0 copy-start.4
  45.1 0.0 collective-permute-done.2.next_ref
  45.1 0.0 copy-start.1
  45.1 1.2 %collective-permute-done.3.prev_ref = f32[408,128]{1,0:T(8,128)S(1)} collective-permute-done((f32[408,128]{1,0:T(8,128)}, f32[408,128]{1,0:T(8,128)S(1)}, u32[]{:S(2)}, u32[]{:S(2)}) %collective-permute-start.3) | collective-permute-done | bytes 208928 | tf_op jit(solution)/shard_map/ppermute | solution.py:263
  46.3 0.0 copy-start.2
  46.3 0.0 all-to-all-done
  46.3 0.0 copy-start
  46.3 0.0 copy-done.5
  46.3 0.0 copy-done.3
  46.3 0.0 copy-done.4
  46.3 0.0 copy-done.1
  46.3 0.6 %copy-done.2 = f32[408,128]{1,0:T(8,128)} copy-done((f32[408,128]{1,0:T(8,128)}, f32[408,128]{1,0:T(8,128)S(1)}, u32[]{:S(2)}) %copy-start.2) | copy-done | bytes 208920
  46.9 0.2 copy-done
  47.2 10.1 %final.1 = f32[3072,256]{1,0:T(8,128)} custom-call(f32[1088,128]{1,0:T(8,128)} %bitcast.9, f32[392,128]{1,0:T(8,128)} %copy-done.3, f32[392,128]{1,0:T(8,128)} %copy-done.4, f32[408,128]{1,0:T(8,128)} %copy-done.1, f32[408,128]{1,0:T(8,128)} %copy-done.2, f32[24,128]{1,0:T(8,128)} %copy-done.5, f32[6160,128]{1,0:T(8,128)} %get-tuple-element.22.placed_in, ...), custom_call_target="tpu_custom_call" | custom-call | flops 1000000000 | bytes 8000000 | tf_op jit(solution)/shard_map/final/pallas_call | solution.py:321
Async XLA Ops:
  7.6 38.7 %all-to-all-start = ((f32[64,1,2176]{2,1,0:T(1,128)}), f32[64,1,2176]{2,1,0:T(1,128)S(1)}, u32[]{:S(2)}, u32[]{:S(2)}) async-start(f32[64,1,2176]{2,1,0:T(1,128)} %bitcast.10), calls=%async_computation | async-start | bytes 1114112 | tf_op jit(solution)/shard_map/all_to_all | solution.py:301
  21.1 23.9 %collective-permute-start.4 = (f32[24,128]{1,0:T(8,128)}, f32[24,128]{1,0:T(8,128)S(1)}, u32[]{:S(2)}, u32[]{:S(2)}) collective-permute-start(f32[24,128]{1,0:T(8,128)} %get-tuple-element.20), channel_id=1, source_target_pairs={{0,128},{64,192},{128,0},{192,64},{1,129},{65,193},{129,1},{193,65... | collective-permute-start | bytes 36872 | tf_op jit(solution)/shard_map/ppermute | solution.py:263
  23.8 21.2 %collective-permute-start = (f32[392,128]{1,0:T(8,128)}, f32[392,128]{1,0:T(8,128)S(1)}, u32[]{:S(2)}, u32[]{:S(2)}) collective-permute-start(f32[392,128]{1,0:T(8,128)} %get-tuple-element.16), channel_id=1, source_target_pairs={{0,1},{1,2},{2,3},{3,4},{4,5},{5,6},{6,7},{7,8},{8,9},{9,10},{10,1... | collective-permute-start | bytes 602120 | tf_op jit(solution)/shard_map/ppermute | solution.py:263
  24.9 20.2 %collective-permute-start.1 = (f32[392,128]{1,0:T(8,128)}, f32[392,128]{1,0:T(8,128)S(1)}, u32[]{:S(2)}, u32[]{:S(2)}) collective-permute-start(f32[392,128]{1,0:T(8,128)} %get-tuple-element.17), channel_id=1, source_target_pairs={{0,63},{1,0},{2,1},{3,2},{4,3},{5,4},{6,5},{7,6},{8,7},{9,8},{10,9... | collective-permute-start | bytes 602120 | tf_op jit(solution)/shard_map/ppermute | solution.py:263
  29.5 15.5 %collective-permute-start.2 = (f32[408,128]{1,0:T(8,128)}, f32[408,128]{1,0:T(8,128)S(1)}, u32[]{:S(2)}, u32[]{:S(2)}) collective-permute-start(f32[408,128]{1,0:T(8,128)} %get-tuple-element.18), channel_id=1, source_target_pairs={{0,64},{64,128},{128,192},{192,0},{1,65},{65,129},{129,193},{193,1... | collective-permute-start | bytes 626696 | tf_op jit(solution)/shard_map/ppermute | solution.py:263
  32.0 14.3 %collective-permute-start.3 = (f32[408,128]{1,0:T(8,128)}, f32[408,128]{1,0:T(8,128)S(1)}, u32[]{:S(2)}, u32[]{:S(2)}) collective-permute-start(f32[408,128]{1,0:T(8,128)} %get-tuple-element.19), channel_id=1, source_target_pairs={{0,192},{64,0},{128,64},{192,128},{1,193},{65,1},{129,65},{193,129... | collective-permute-start | bytes 626696 | tf_op jit(solution)/shard_map/ppermute | solution.py:263
  45.0 1.3 %copy-start.5 = (f32[24,128]{1,0:T(8,128)}, f32[24,128]{1,0:T(8,128)S(1)}, u32[]{:S(2)}) copy-start(f32[24,128]{1,0:T(8,128)S(1)} %collective-permute-done.4.far_ref) | copy-start | bytes 36868
  45.0 1.2 %copy-start.3 = (f32[392,128]{1,0:T(8,128)}, f32[392,128]{1,0:T(8,128)S(1)}, u32[]{:S(2)}) copy-start(f32[392,128]{1,0:T(8,128)S(1)} %collective-permute-done.up_ref) | copy-start | bytes 602116
  45.1 1.2 %copy-start.4 = (f32[392,128]{1,0:T(8,128)}, f32[392,128]{1,0:T(8,128)S(1)}, u32[]{:S(2)}) copy-start(f32[392,128]{1,0:T(8,128)S(1)} %collective-permute-done.1.down_ref) | copy-start | bytes 602116
  45.1 1.2 %copy-start.1 = (f32[408,128]{1,0:T(8,128)}, f32[408,128]{1,0:T(8,128)S(1)}, u32[]{:S(2)}) copy-start(f32[408,128]{1,0:T(8,128)S(1)} %collective-permute-done.2.next_ref) | copy-start | bytes 626692
  46.3 0.7 %copy-start.2 = (f32[408,128]{1,0:T(8,128)}, f32[408,128]{1,0:T(8,128)S(1)}, u32[]{:S(2)}) copy-start(f32[408,128]{1,0:T(8,128)S(1)} %collective-permute-done.3.prev_ref) | copy-start | bytes 626692
  46.3 0.9 %copy-start = (f32[64,1,2176]{2,1,0:T(1,128)}, f32[64,1,2176]{2,1,0:T(1,128)S(1)}, u32[]{:S(2)}) copy-start(f32[64,1,2176]{2,1,0:T(1,128)S(1)} %all-to-all-done) | copy-start | bytes 1671172

commit v2 on v1

v2 whole, which is shorter than its diff:
```python
import jax
import jax.numpy as jnp
from jax import lax
from jax.experimental import pallas as pl
from jax.experimental.pallas import tpu as pltpu
from jax.sharding import PartitionSpec as P


SPREAD = 8
MOST = 192
COLUMNS = 3072
BLOCKS = COLUMNS // 128
WIDTH = 256
N_COMP = 64
N_IO = 4
PACKET = 2 * SPREAD + 1
NEAR_COMP = MOST
NEAR_IO = MOST + SPREAD
COMP_ROWS = 392
IO_ROWS = 408
FAR_ROWS = 24
KEYS = 80
DUMP = COLUMNS
SIZES = (512, 512, 512, 512, 512, 256, 128, 128)
PLACED = 2 * (COLUMNS + 8)
VMEM = pltpu.VMEM
SMEM = pltpu.SMEM


def coordinates():
    return lax.axis_index("io"), lax.axis_index("comp")


def pack_kernel(
    offsets_ref,
    fields_ref,
    spread_out,
    up_ref,
    down_ref,
    next_ref,
    prev_ref,
    far_ref,
    stay_ref,
    fields,
    offsets,
    spread_ref,
    onehot,
    prefix,
    ranks,
    high,
    low,
    source,
    source_s,
    sems,
):
    fetch_offsets = pltpu.make_async_copy(offsets_ref, offsets, sems.at[2])
    fetch_offsets.start()
    fetch = pltpu.make_async_copy(fields_ref, fields, sems.at[0])
    fetch.start()
    fetch_offsets.wait()
    group, task = coordinates()
    offset = offsets[...]
    owner = ((offset >> 10) * 21846) >> 16
    position = offset - owner * COLUMNS
    owner_group = owner >> 6
    owner_task = owner & (N_COMP - 1)
    along_comp = (owner_group == group) & (owner_task != task)
    along_io = (owner_task == task) & (owner_group != group)
    key = jnp.where(along_comp, owner_task, jnp.where(along_io, N_COMP + owner_group, 127))
    rows = lax.broadcasted_iota(jnp.int32, (KEYS, 128), 0)
    for b in range(BLOCKS):
        hit = rows == key[b : b + 1, :]
        onehot[b * KEYS : (b + 1) * KEYS, :] = jnp.where(hit, 1.0, 0.0).astype(jnp.bfloat16)
    r = lax.broadcasted_iota(jnp.int32, (128, 256), 0)
    c = lax.broadcasted_iota(jnp.int32, (128, 256), 1)
    earlier = jnp.where((r < c) | (c >= 128), 1.0, 0.0).astype(jnp.bfloat16)
    prefix[...] = jnp.dot(onehot[...], earlier, preferred_element_type=jnp.float32)
    carry = jnp.zeros((KEYS, 128), jnp.float32)
    for b in range(BLOCKS):
        hit = rows == key[b : b + 1, :]
        counted = prefix[b * KEYS : (b + 1) * KEYS, 0:128] + carry
        ranks[b : b + 1, :] = jnp.sum(jnp.where(hit, counted, 0.0), axis=0, keepdims=True)
        carry = carry + prefix[b * KEYS : (b + 1) * KEYS, 128:256]
    rank = ranks[...].astype(jnp.int32)
    upper = (task + 1) & (N_COMP - 1)
    after = (group + 1) & (N_IO - 1)
    before = (group + N_IO - 1) & (N_IO - 1)
    comp_slot = jnp.where(
        rank < SPREAD,
        owner_task * SPREAD + rank,
        jnp.where(owner_task == upper, 512, 768) + rank - SPREAD,
    )
    io_slot = (
        jnp.where(owner_group == after, 1024, jnp.where(owner_group == before, 1280, 1536)) + rank
    )
    slot = jnp.where(along_comp, comp_slot, jnp.where(along_io, io_slot, 2047))
    stay_ref[...] = 2 * jnp.where(along_comp | along_io, DUMP, position)
    slot_high = slot >> 7
    slot_low = slot & 127
    column = lax.broadcasted_iota(jnp.int32, (BLOCKS, 128), 0) * 128 + lax.broadcasted_iota(
        jnp.int32, (BLOCKS, 128), 1
    )
    coded = position + 1
    parts = [
        (column & 255).astype(jnp.float32),
        (column >> 8).astype(jnp.float32),
        (coded & 255).astype(jnp.float32),
        (coded >> 8).astype(jnp.float32),
    ]
    rows16 = lax.broadcasted_iota(jnp.int32, (16, 128), 0)
    rows128 = lax.broadcasted_iota(jnp.int32, (128, 128), 0)
    for b in range(BLOCKS):
        hit = rows16 == slot_high[b : b + 1, :]
        for j in range(4):
            high[16 * j : 16 * (j + 1), 128 * b : 128 * (b + 1)] = jnp.where(
                hit, parts[j][b : b + 1, :], 0.0
            ).astype(jnp.bfloat16)
        low[:, 128 * b : 128 * (b + 1)] = jnp.where(
            rows128 == slot_low[b : b + 1, :], 1.0, 0.0
        ).astype(jnp.bfloat16)
    found = lax.dot_general(
        high[...], low[...], (((1,), (1,)), ((), ())), preferred_element_type=jnp.float32
    )
    chosen = (found[0:16, :] + 256.0 * found[16:32, :]).astype(jnp.int32)
    source[...] = (chosen >> 3) * 16 + (chosen & 7)
    push = pltpu.make_async_copy(source, source_s, sems.at[1])
    push.start()
    coded = found[32:48, :] + 256.0 * found[48:64, :]
    goal = 2.0 * jnp.where(coded > 0.5, coded - 1.0, float(DUMP))
    turned = pltpu.roll(goal, (task & 15) * SPREAD, 1)
    for j in range(16):
        row = pltpu.roll(turned, (128 - SPREAD * j) % 128, 1)
        for g in range(N_COMP // 16):
            at = PACKET * (16 * g + j) + 2 * SPREAD
            spread_ref[at : at + 1, :] = row[g : g + 1, :]
    up_ref[0:2, :] = goal[4:6, :]
    down_ref[0:2, :] = goal[6:8, :]
    next_ref[0:2, :] = goal[8:10, :]
    prev_ref[0:2, :] = goal[10:12, :]
    far_ref[0:1, :] = goal[12:13, :]
    push.wait()
    fetch.wait()

    def copy(into, at, slot):
        row = source_s[slot // 128, slot % 128]
        into[pl.ds(at, 1), :] = fields[pl.ds(row, 1), :]
        into[pl.ds(at + 1, 1), :] = fields[pl.ds(row + 8, 1), :]

    part = N_COMP * PACKET // 4
    writes = []
    for q in range(4):
        for s in range(128 * q, 128 * (q + 1)):
            copy(spread_ref, PACKET * (s // SPREAD) + 2 * (s % SPREAD), s)
        write = pltpu.make_async_copy(
            spread_ref.at[pl.ds(part * q, part), :],
            spread_out.at[pl.ds(part * q, part), :],
            sems.at[3 + q],
        )
        write.start()
        writes.append(write)
    for s in range(NEAR_COMP):
        copy(up_ref, 2 + 2 * s, 512 + s)
    for s in range(NEAR_COMP):
        copy(down_ref, 2 + 2 * s, 768 + s)
    for s in range(NEAR_IO):
        copy(next_ref, 2 + 2 * s, 1024 + s)
    for s in range(NEAR_IO):
        copy(prev_ref, 2 + 2 * s, 1280 + s)
    for s in range(SPREAD):
        copy(far_ref, 1 + 2 * s, 1536 + s)
    for write in writes:
        write.wait()


def local_kernel(stay_ref, fields_in, remap_ref, placed_ref, high_ref, low_ref, fields_ref, sems):
    part = 2 * COLUMNS // 4
    fetches = []
    for q in range(4):
        fetch = pltpu.make_async_copy(
            fields_in.at[pl.ds(part * q, part), :],
            fields_ref.at[pl.ds(part * q, part), :],
            sems.at[q],
        )
        fetch.start()
        fetches.append(fetch)
    zero = jnp.zeros((64, 64), jnp.float32)
    for f in range(4):
        band = jnp.concatenate([remap_ref[f] if g == f else zero for g in range(4)], axis=1)
        top = band.astype(jnp.bfloat16)
        high_ref[64 * f : 64 * (f + 1), :] = top
        low_ref[64 * f : 64 * (f + 1), :] = (band - top.astype(jnp.float32)).astype(jnp.bfloat16)

    def step(i, _):
        for k in range(128):
            at = stay_ref[i, k]
            row = 256 * i + 16 * (k // 8) + k % 8
            placed_ref[pl.ds(at, 1), :] = fields_ref[pl.ds(row, 1), :]
            placed_ref[pl.ds(at + 1, 1), :] = fields_ref[pl.ds(row + 8, 1), :]
        return 0

    for q, fetch in enumerate(fetches):
        fetch.wait()
        lax.fori_loop(BLOCKS // 4 * q, BLOCKS // 4 * (q + 1), step, 0)


def final_kernel(
    spread_ref,
    up_ref,
    down_ref,
    next_ref,
    prev_ref,
    far_ref,
    placed_in,
    high_ref,
    low_ref,
    out_ref,
    placed,
    goal,
    goal_s,
    result,
    sems,
):
    fetch = pltpu.make_async_copy(placed_in, placed, sems.at[1])
    fetch.start()
    rows = jnp.concatenate(
        [spread_ref[PACKET * t + 2 * SPREAD : PACKET * (t + 1), :] for t in range(N_COMP)], axis=0
    )
    packet = lax.broadcasted_iota(jnp.int32, (N_COMP, 128), 0)
    lane = lax.broadcasted_iota(jnp.int32, (N_COMP, 128), 1)
    rows = jnp.where((packet & 15) == (lane >> 3), rows, 0.0)
    goal[0:4, :] = jnp.sum(rows.reshape(4, 16, 128), axis=1).astype(jnp.int32)
    for j, ref in enumerate((up_ref, down_ref, next_ref, prev_ref)):
        goal[4 + 2 * j : 6 + 2 * j, :] = ref[0:2, :].astype(jnp.int32)
    goal[12:13, :] = far_ref[0:1, :].astype(jnp.int32)
    push = pltpu.make_async_copy(goal, goal_s, sems.at[0])
    push.start()
    push.wait()
    fetch.wait()

    def copy(origin, at, slot):
        to = goal_s[slot // 128, slot % 128]
        placed[pl.ds(to, 1), :] = origin[pl.ds(at, 1), :]
        placed[pl.ds(to + 1, 1), :] = origin[pl.ds(at + 1, 1), :]

    for s in range(N_COMP * SPREAD):
        copy(spread_ref, PACKET * (s // SPREAD) + 2 * (s % SPREAD), s)
    for s in range(NEAR_COMP):
        copy(up_ref, 2 + 2 * s, 512 + s)
    for s in range(NEAR_COMP):
        copy(down_ref, 2 + 2 * s, 768 + s)
    for s in range(NEAR_IO):
        copy(next_ref, 2 + 2 * s, 1024 + s)
    for s in range(NEAR_IO):
        copy(prev_ref, 2 + 2 * s, 1280 + s)
    for s in range(SPREAD):
        copy(far_ref, 1 + 2 * s, 1536 + s)

    copies = []
    start = 0
    for j, size in enumerate(SIZES):
        left = placed[pl.ds(2 * start, size, stride=2), :]
        right = placed[pl.ds(2 * start + 1, size, stride=2), :]
        x = jnp.concatenate([left, right], axis=1)
        x_high = x.astype(jnp.bfloat16)
        x_low = (x - x_high.astype(jnp.float32)).astype(jnp.bfloat16)
        total = jnp.dot(x_high, high_ref[...], preferred_element_type=jnp.float32)
        total += jnp.dot(x_high, low_ref[...], preferred_element_type=jnp.float32)
        total += jnp.dot(x_low, high_ref[...], preferred_element_type=jnp.float32)
        result[start : start + size, :] = total
        write = pltpu.make_async_copy(
            result.at[pl.ds(start, size), :], out_ref.at[pl.ds(start, size), :], sems.at[2 + j]
        )
        write.start()
        copies.append(write)
        start += size
    for write in copies:
        write.wait()


def shift(value, axis, by):
    peers = lax.axis_size(axis)
    return lax.ppermute(value, axis, [(i, (i + by) % peers) for i in range(peers)])


def per_device(fields, file_offset, level_remap):
    f32 = jnp.float32
    whole = pl.BlockSpec(memory_space=VMEM)
    anywhere = pl.BlockSpec(memory_space=pl.ANY)
    scalars = pl.BlockSpec(memory_space=SMEM)
    fields = (
        fields.reshape(COLUMNS // 8, 8, 2, 128).transpose(0, 2, 1, 3).reshape(2 * COLUMNS, 128)
    )
    fields = pltpu.with_memory_space_constraint(fields, pltpu.HBM)
    file_offset = pltpu.with_memory_space_constraint(file_offset, pltpu.HBM)
    spread, up, down, after, before, far, stay = pl.pallas_call(
        pack_kernel,
        name="pack",
        out_shape=[
            pltpu.HBM((N_COMP * PACKET, 128), f32),
            VMEM((COMP_ROWS, 128), f32),
            VMEM((COMP_ROWS, 128), f32),
            VMEM((IO_ROWS, 128), f32),
            VMEM((IO_ROWS, 128), f32),
            VMEM((FAR_ROWS, 128), f32),
            pltpu.HBM((BLOCKS, 128), jnp.int32),
        ],
        in_specs=[anywhere, anywhere],
        out_specs=[anywhere] + [whole] * 6,
        scratch_shapes=[
            VMEM((2 * COLUMNS, 128), f32),
            VMEM((BLOCKS, 128), jnp.int32),
            VMEM((N_COMP * PACKET, 128), f32),
            VMEM((BLOCKS * KEYS, 128), jnp.bfloat16),
            VMEM((BLOCKS * KEYS, 256), f32),
            VMEM((BLOCKS, 128), f32),
            VMEM((64, COLUMNS), jnp.bfloat16),
            VMEM((128, COLUMNS), jnp.bfloat16),
            VMEM((16, 128), jnp.int32),
            SMEM((16, 128), jnp.int32),
            pltpu.SemaphoreType.DMA((7,)),
        ],
        compiler_params=pltpu.CompilerParams(vmem_limit_bytes=40 * 2**20),
        cost_estimate=pl.CostEstimate(flops=20_000_000, bytes_accessed=5_000_000, transcendentals=0),
    )(file_offset, fields)
    spread = lax.all_to_all(
        spread.reshape(N_COMP, 1, PACKET * 128), "comp", split_axis=0, concat_axis=0, tiled=True
    ).reshape(N_COMP * PACKET, 128)
    up = shift(up, "comp", 1)
    down = shift(down, "comp", -1)
    after = shift(after, "io", 1)
    before = shift(before, "io", -1)
    far = shift(far, "io", 2)
    placed, high, low = pl.pallas_call(
        local_kernel,
        name="local",
        out_shape=[
            pltpu.HBM((PLACED, 128), f32),
            VMEM((WIDTH, WIDTH), jnp.bfloat16),
            VMEM((WIDTH, WIDTH), jnp.bfloat16),
        ],
        in_specs=[scalars, anywhere, whole],
        out_specs=[whole] * 3,
        scratch_shapes=[VMEM((2 * COLUMNS, 128), f32), pltpu.SemaphoreType.DMA((4,))],
        compiler_params=pltpu.CompilerParams(vmem_limit_bytes=40 * 2**20),
        cost_estimate=pl.CostEstimate(flops=4_000_000_000, bytes_accessed=6_000_000, transcendentals=0),
    )(stay, fields, level_remap)
    operands = [
        pltpu.with_memory_space_constraint(x, VMEM)
        for x in (spread, up, down, after, before, far, high, low)
    ]
    operands.insert(6, pltpu.with_memory_space_constraint(placed, pltpu.HBM))
    return pl.pallas_call(
        final_kernel,
        name="final",
        out_shape=jax.ShapeDtypeStruct((COLUMNS, WIDTH), f32),
        in_specs=[whole] * 6 + [anywhere, whole, whole],
        out_specs=anywhere,
        scratch_shapes=[
            VMEM((PLACED, 128), f32),
            VMEM((16, 128), jnp.int32),
            SMEM((16, 128), jnp.int32),
            VMEM((COLUMNS, WIDTH), f32),
            pltpu.SemaphoreType.DMA((2 + len(SIZES),)),
        ],
        compiler_params=pltpu.CompilerParams(vmem_limit_bytes=40 * 2**20),
        cost_estimate=pl.CostEstimate(flops=1_000_000_000, bytes_accessed=8_000_000, transcendentals=0),
    )(*operands)


def solution(mesh):
    placed = (P(("io", "comp"), None), P(("io", "comp"), None), P())

    return jax.shard_map(
        per_device, mesh=mesh, in_specs=placed, out_specs=P(("io", "comp"), None), check_vma=False
    )
```

time: 57.6 us -> 48.5 us (0.84)
  Pallas kernels: 30.7 us -> 16.2 us
  waiting for transfers between devices: 1.2 us -> 6.96 us
    pallas_call x2, Pallas kernels: 20.6 us -> 11 us  [the longest x1 6.49 us: per_device(): pl.pallas_call(local_kernel, name='local', out_shape=[pltpu.HBM((PLACED,...]
    ppermute x5, waiting for transfers between devices: 1.19 us -> 6.96 us  [shift(): lax.ppermute(value, axis, [(i, (i + by) % peers) for i in range(peers)])]
    pallas_call x1, Pallas kernels: 10.1 us -> 5.16 us  [per_device(): pl.pallas_call(final_kernel, name='final', out_shape=jax.ShapeDtypeStruct...]
  transfers between devices with their start and end apart: 6 -> 6, of which waited for: 1 -> 2; matrix products, arithmetic and copies ran while one was open for 0% -> 0% of each run, Pallas kernels for 23% -> 13%
where the time goes in v2:
time: 48.5 us; the launch traced here: 48.3 us
  starting transfers between devices  24.4 us (50%)
  Pallas kernels  16.2 us (33%)
  waiting for transfers between devices  6.96 us (14%)
  local copies, waits for them, and re-layouts  0.71 us (1%)
    all_to_all x1, starting transfers between devices, per_device(): lax.all_to_all(spread.reshape(N_COMP, 1, PACKET * 128), 'comp', split_axi...  13.5 us
    ppermute x5, starting transfers between devices, shift(): lax.ppermute(value, axis, [(i, (i + by) % peers) for i in range(peers)])  10.9 us
    ppermute x5, waiting for transfers between devices, shift(): lax.ppermute(value, axis, [(i, (i + by) % peers) for i in range(peers)])  6.96 us
    pallas_call x1, Pallas kernels, per_device(): pl.pallas_call(local_kernel, name='local', out_shape=[pltpu.HBM((PLACED,...  6.49 us
    pallas_call x1, Pallas kernels, per_device(): pl.pallas_call(final_kernel, name='final', out_shape=jax.ShapeDtypeStruct...  5.16 us
    pallas_call x1, Pallas kernels, per_device(): pl.pallas_call(pack_kernel, name='pack', out_shape=[pltpu.HBM((N_COMP * P...  4.51 us
  transfers between devices with their start and end apart: 6, of which 2 were waited for; matrix products, arithmetic and copies ran while one was open for 0% of the time, Pallas kernels for 13%

profile of v2, /device:TPU:1, one launch (start us, length us, event | category | flops | bytes accessed | tf_op | source)
XLA Modules:
  0.0 48.3 jit_solution(2662030087346725599)
XLA Ops:
  0.0 0.0 copy-start
  0.0 4.5 %pack.1 = (f32[1088,128]{1,0:T(8,128)}, f32[392,128]{1,0:T(8,128)S(1)}, f32[392,128]{1,0:T(8,128)S(1)}, f32[408,128]{1,0:T(8,128)S(1)}, f32[408,128]{1,0:T(8,128...) custom-call(s32[24,128]{1,0:T(8,128)} %offsets_ref.1, f32[6144,128]{1,0:T(8,128)} %bitcast.8), custom_call_target="tpu_custom_call" | custom-call | flops 20000000 | bytes 5000000 | tf_op jit(solution)/shard_map/pack/pallas_call | solution.py:295
  4.5 13.5 %all-to-all-start = ((f32[64,1,2176]{2,1,0:T(1,128)}), f32[64,1,2176]{2,1,0:T(1,128)S(1)}, u32[]{:S(2)}, u32[]{:S(2)}) async-start(f32[64,1,2176]{2,1,0:T(1,128)} %bitcast.10), calls=%async_computation | async-start | bytes 1114112 | tf_op jit(solution)/shard_map/all_to_all | solution.py:325
  18.0 2.7 %collective-permute-start.4 = (f32[24,128]{1,0:T(8,128)S(1)}, f32[24,128]{1,0:T(8,128)S(1)}, u32[]{:S(2)}, u32[]{:S(2)}) collective-permute-start(f32[24,128]{1,0:T(8,128)S(1)} %get-tuple-element.20), channel_id=1, source_target_pairs={{0,128},{64,192},{128,0},{192,64},{1,129},{65,193},{129,1},{193,65... | collective-permute-start | bytes 36872 | tf_op jit(solution)/shard_map/ppermute | solution.py:282
  20.7 1.0 %collective-permute-start = (f32[392,128]{1,0:T(8,128)S(1)}, f32[392,128]{1,0:T(8,128)S(1)}, u32[]{:S(2)}, u32[]{:S(2)}) collective-permute-start(f32[392,128]{1,0:T(8,128)S(1)} %get-tuple-element.16), channel_id=1, source_target_pairs={{0,1},{1,2},{2,3},{3,4},{4,5},{5,6},{6,7},{7,8},{8,9},{9,10},{10,1... | collective-permute-start | bytes 602120 | tf_op jit(solution)/shard_map/ppermute | solution.py:282
  21.7 4.7 %collective-permute-start.1 = (f32[392,128]{1,0:T(8,128)S(1)}, f32[392,128]{1,0:T(8,128)S(1)}, u32[]{:S(2)}, u32[]{:S(2)}) collective-permute-start(f32[392,128]{1,0:T(8,128)S(1)} %get-tuple-element.17), channel_id=1, source_target_pairs={{0,63},{1,0},{2,1},{3,2},{4,3},{5,4},{6,5},{7,6},{8,7},{9,8},{10,9... | collective-permute-start | bytes 602120 | tf_op jit(solution)/shard_map/ppermute | solution.py:282
  26.4 2.5 %collective-permute-start.2 = (f32[408,128]{1,0:T(8,128)S(1)}, f32[408,128]{1,0:T(8,128)S(1)}, u32[]{:S(2)}, u32[]{:S(2)}) collective-permute-start(f32[408,128]{1,0:T(8,128)S(1)} %get-tuple-element.18), channel_id=1, source_target_pairs={{0,64},{64,128},{128,192},{192,0},{1,65},{65,129},{129,193},{193,1... | collective-permute-start | bytes 626696 | tf_op jit(solution)/shard_map/ppermute | solution.py:282
  28.9 0.0 collective-permute-start.3
  28.9 0.0 copy-done
  28.9 0.0 copy-start.1
  28.9 0.7 %copy-done.1 = s32[24,128]{1,0:T(8,128)S(1)} copy-done((s32[24,128]{1,0:T(8,128)S(1)}, s32[24,128]{1,0:T(8,128)}, u32[]{:S(2)}) %copy-start.1) | copy-done | bytes 12312
  29.6 6.5 %local.1 = (f32[6160,128]{1,0:T(8,128)}, bf16[256,256]{1,0:T(8,128)(2,1)S(1)}, bf16[256,256]{1,0:T(8,128)(2,1)S(1)}) custom-call(s32[24,128]{1,0:T(8,128)S(1)} %copy-done.1, f32[6144,128]{1,0:T(8,128)} %bitcast.9, f32[4,64,64]{2,1,0:T(8,128)S(1)} %copy-done), custom_call_target="tpu_custom_call" | custom-call | flops 4000000000 | bytes 6000000 | tf_op jit(solution)/shard_map/local/pallas_call | solution.py:333
  36.1 0.0 collective-permute-done.4.far_ref
  36.1 3.7 %collective-permute-done.up_ref = f32[392,128]{1,0:T(8,128)S(1)} collective-permute-done((f32[392,128]{1,0:T(8,128)S(1)}, f32[392,128]{1,0:T(8,128)S(1)}, u32[]{:S(2)}, u32[]{:S(2)}) %collective-permute-start) | collective-permute-done | bytes 200736 | tf_op jit(solution)/shard_map/ppermute | solution.py:282
  39.9 0.0 collective-permute-done.1.down_ref
  39.9 0.0 collective-permute-done.2.next_ref
  39.9 3.2 %collective-permute-done.3.prev_ref = f32[408,128]{1,0:T(8,128)S(1)} collective-permute-done((f32[408,128]{1,0:T(8,128)S(1)}, f32[408,128]{1,0:T(8,128)S(1)}, u32[]{:S(2)}, u32[]{:S(2)}) %collective-permute-start.3) | collective-permute-done | bytes 208928 | tf_op jit(solution)/shard_map/ppermute | solution.py:282
  43.1 0.0 all-to-all-done
  43.1 5.2 %final.1 = f32[3072,256]{1,0:T(8,128)} custom-call(f32[1088,128]{1,0:T(8,128)S(1)} %bitcast.7, f32[392,128]{1,0:T(8,128)S(1)} %collective-permute-done.up_ref, f32[392,128]{1,0:T(8,128)S(1)} %collective-permute-done.1.down_ref, f32[408,128]{1,0:T(8,128)S(1)} %collective-permute-done.2.next_ref, f32[408,128]{1,0:T(8,128)S(1)} %collective-permute-done.3.prev_ref, ...), custom_call_target="tpu_custom_call" | custom-call | flops 1000000000 | bytes 8000000 | tf_op jit(solution)/shard_map/final/pallas_call | solution.py:352
Async XLA Ops:
  0.0 28.9 %copy-start = (f32[4,64,64]{2,1,0:T(8,128)S(1)}, f32[4,64,64]{2,1,0:T(8,128)}, u32[]{:S(2)}) copy-start(f32[4,64,64]{2,1,0:T(8,128)} %remap_ref.1) | copy-start | bytes 196612
  4.5 38.6 %all-to-all-start = ((f32[64,1,2176]{2,1,0:T(1,128)}), f32[64,1,2176]{2,1,0:T(1,128)S(1)}, u32[]{:S(2)}, u32[]{:S(2)}) async-start(f32[64,1,2176]{2,1,0:T(1,128)} %bitcast.10), calls=%async_computation | async-start | bytes 1114112 | tf_op jit(solution)/shard_map/all_to_all | solution.py:325
  18.0 18.1 %collective-permute-start.4 = (f32[24,128]{1,0:T(8,128)S(1)}, f32[24,128]{1,0:T(8,128)S(1)}, u32[]{:S(2)}, u32[]{:S(2)}) collective-permute-start(f32[24,128]{1,0:T(8,128)S(1)} %get-tuple-element.20), channel_id=1, source_target_pairs={{0,128},{64,192},{128,0},{192,64},{1,129},{65,193},{129,1},{193,65... | collective-permute-start | bytes 36872 | tf_op jit(solution)/shard_map/ppermute | solution.py:282
  20.7 19.1 %collective-permute-start = (f32[392,128]{1,0:T(8,128)S(1)}, f32[392,128]{1,0:T(8,128)S(1)}, u32[]{:S(2)}, u32[]{:S(2)}) collective-permute-start(f32[392,128]{1,0:T(8,128)S(1)} %get-tuple-element.16), channel_id=1, source_target_pairs={{0,1},{1,2},{2,3},{3,4},{4,5},{5,6},{6,7},{7,8},{8,9},{9,10},{10,1... | collective-permute-start | bytes 602120 | tf_op jit(solution)/shard_map/ppermute | solution.py:282
  21.7 18.1 %collective-permute-start.1 = (f32[392,128]{1,0:T(8,128)S(1)}, f32[392,128]{1,0:T(8,128)S(1)}, u32[]{:S(2)}, u32[]{:S(2)}) collective-permute-start(f32[392,128]{1,0:T(8,128)S(1)} %get-tuple-element.17), channel_id=1, source_target_pairs={{0,63},{1,0},{2,1},{3,2},{4,3},{5,4},{6,5},{7,6},{8,7},{9,8},{10,9... | collective-permute-start | bytes 602120 | tf_op jit(solution)/shard_map/ppermute | solution.py:282
  26.4 13.4 %collective-permute-start.2 = (f32[408,128]{1,0:T(8,128)S(1)}, f32[408,128]{1,0:T(8,128)S(1)}, u32[]{:S(2)}, u32[]{:S(2)}) collective-permute-start(f32[408,128]{1,0:T(8,128)S(1)} %get-tuple-element.18), channel_id=1, source_target_pairs={{0,64},{64,128},{128,192},{192,0},{1,65},{65,129},{129,193},{193,1... | collective-permute-start | bytes 626696 | tf_op jit(solution)/shard_map/ppermute | solution.py:282
  28.9 14.2 %collective-permute-start.3 = (f32[408,128]{1,0:T(8,128)S(1)}, f32[408,128]{1,0:T(8,128)S(1)}, u32[]{:S(2)}, u32[]{:S(2)}) collective-permute-start(f32[408,128]{1,0:T(8,128)S(1)} %get-tuple-element.19), channel_id=1, source_target_pairs={{0,192},{64,0},{128,64},{192,128},{1,193},{65,1},{129,65},{193,129... | collective-permute-start | bytes 626696 | tf_op jit(solution)/shard_map/ppermute | solution.py:282
  28.9 0.7 %copy-start.1 = (s32[24,128]{1,0:T(8,128)S(1)}, s32[24,128]{1,0:T(8,128)}, u32[]{:S(2)}) copy-start(s32[24,128]{1,0:T(8,128)} %get-tuple-element.21.stay_ref) | copy-start | bytes 36868

commit v3 on v2

--- a/solution.py
+++ b/solution.py
@@ -21,7 +21,7 @@
 FAR_ROWS = 24
 KEYS = 80
 DUMP = COLUMNS
-SIZES = (512, 512, 512, 512, 512, 256, 128, 128)
+RECEIVED = N_COMP * SPREAD + 2 * NEAR_COMP + 2 * NEAR_IO + SPREAD
 PLACED = 2 * (COLUMNS + 8)
 VMEM = pltpu.VMEM
 SMEM = pltpu.SMEM
@@ -126,7 +126,8 @@
     push = pltpu.make_async_copy(source, source_s, sems.at[1])
     push.start()
     coded = found[32:48, :] + 256.0 * found[48:64, :]
-    goal = 2.0 * jnp.where(coded > 0.5, coded - 1.0, float(DUMP))
+    goal = jnp.where(coded > 0.5, coded - 1.0, float(DUMP)).astype(jnp.int32)
+    goal = ((goal >> 3) * 16 + (goal & 7)).astype(jnp.float32)
     turned = pltpu.roll(goal, (task & 15) * SPREAD, 1)
     for j in range(16):
         row = pltpu.roll(turned, (128 - SPREAD * j) % 128, 1)
@@ -143,8 +144,7 @@
 
     def copy(into, at, slot):
         row = source_s[slot // 128, slot % 128]
-        into[pl.ds(at, 1), :] = fields[pl.ds(row, 1), :]
-        into[pl.ds(at + 1, 1), :] = fields[pl.ds(row + 8, 1), :]
+        into[pl.ds(at, 2), :] = fields[pl.ds(row, 2, stride=8), :]
 
     part = N_COMP * PACKET // 4
     writes = []
@@ -172,13 +172,26 @@
         write.wait()
 
 
-def local_kernel(stay_ref, fields_in, remap_ref, placed_ref, high_ref, low_ref, fields_ref, sems):
+def remap(x, high_ref, low_ref):
+    x_high = x.astype(jnp.bfloat16)
+    x_low = (x - x_high.astype(jnp.float32)).astype(jnp.bfloat16)
+    total = jnp.dot(x_high, high_ref[...], preferred_element_type=jnp.float32)
+    total += jnp.dot(x_high, low_ref[...], preferred_element_type=jnp.float32)
+    total += jnp.dot(x_low, high_ref[...], preferred_element_type=jnp.float32)
+    return total
+
+
+def local_kernel(
+    stay_in, fields_in, remap_ref, kept_ref, high_ref, low_ref, fields, placed, result, stay, sems
+):
+    fetch_stay = pltpu.make_async_copy(stay_in, stay, sems.at[4])
+    fetch_stay.start()
     part = 2 * COLUMNS // 4
     fetches = []
     for q in range(4):
         fetch = pltpu.make_async_copy(
             fields_in.at[pl.ds(part * q, part), :],
-            fields_ref.at[pl.ds(part * q, part), :],
+            fields.at[pl.ds(part * q, part), :],
             sems.at[q],
         )
         fetch.start()
@@ -189,18 +202,29 @@
         top = band.astype(jnp.bfloat16)
         high_ref[64 * f : 64 * (f + 1), :] = top
         low_ref[64 * f : 64 * (f + 1), :] = (band - top.astype(jnp.float32)).astype(jnp.bfloat16)
-
-    def step(i, _):
-        for k in range(128):
-            at = stay_ref[i, k]
-            row = 256 * i + 16 * (k // 8) + k % 8
-            placed_ref[pl.ds(at, 1), :] = fields_ref[pl.ds(row, 1), :]
-            placed_ref[pl.ds(at + 1, 1), :] = fields_ref[pl.ds(row + 8, 1), :]
-        return 0
-
+    fetch_stay.wait()
     for q, fetch in enumerate(fetches):
         fetch.wait()
-        lax.fori_loop(BLOCKS // 4 * q, BLOCKS // 4 * (q + 1), step, 0)
+        for c in range(COLUMNS // 4 * q, COLUMNS // 4 * (q + 1)):
+            row = 16 * (c // 8) + c % 8
+            placed[pl.ds(stay[c // 128, c % 128], 2), :] = fields[pl.ds(row, 2, stride=8), :]
+    writes = []
+    size = 512
+    for j in range(COLUMNS // size):
+        left = placed[pl.ds(2 * size * j, size, stride=2), :]
+        right = placed[pl.ds(2 * size * j + 1, size, stride=2), :]
+        result[size * j : size * (j + 1), :] = remap(
+            jnp.concatenate([left, right], axis=1), high_ref, low_ref
+        )
+        write = pltpu.make_async_copy(
+            result.at[pl.ds(size * j, size), :],
+            kept_ref.at[pl.ds(size * j, size), :],
+            sems.at[5 + j],
+        )
+        write.start()
+        writes.append(write)
+    for write in writes:
+        write.wait()
 
 
 def final_kernel(
@@ -210,18 +234,24 @@
     next_ref,
     prev_ref,
     far_ref,
-    placed_in,
+    kept_in,
     high_ref,
     low_ref,
     out_ref,
-    placed,
+    kept,
     goal,
     goal_s,
-    result,
+    mixed,
     sems,
 ):
-    fetch = pltpu.make_async_copy(placed_in, placed, sems.at[1])
-    fetch.start()
+    part = 2 * COLUMNS // 4
+    fetches = []
+    for q in range(4):
+        fetch = pltpu.make_async_copy(
+            kept_in.at[pl.ds(part * q, part), :], kept.at[pl.ds(part * q, part), :], sems.at[1 + q]
+        )
+        fetch.start()
+        fetches.append(fetch)
     rows = jnp.concatenate(
         [spread_ref[PACKET * t + 2 * SPREAD : PACKET * (t + 1), :] for t in range(N_COMP)], axis=0
     )
@@ -234,46 +264,50 @@
     goal[12:13, :] = far_ref[0:1, :].astype(jnp.int32)
     push = pltpu.make_async_copy(goal, goal_s, sems.at[0])
     push.start()
+
+    def halves(ref, first, count, stride, step):
+        return jnp.concatenate(
+            [ref[pl.ds(first, count, stride=stride), :], ref[pl.ds(first + step, count, stride=stride), :]],
+            axis=1,
+        )
+
+    groups = [
+        [halves(spread_ref, 2 * k, N_COMP, PACKET, 1) for k in range(SPREAD)],
+        [halves(ref, 2, NEAR_COMP, 2, 1) for ref in (up_ref, down_ref)],
+        [halves(ref, 2, NEAR_IO, 2, 1) for ref in (next_ref, prev_ref)]
+        + [halves(far_ref, 1, SPREAD, 2, 1)],
+    ]
+    at = 0
+    for group in groups:
+        total = remap(jnp.concatenate(group, axis=0), high_ref, low_ref)
+        for g in range(total.shape[0] // 8):
+            mixed[at : at + 8, :] = total[8 * g : 8 * (g + 1), 0:128]
+            mixed[at + 8 : at + 16, :] = total[8 * g : 8 * (g + 1), 128:256]
+            at += 16
     push.wait()
-    fetch.wait()
-
-    def copy(origin, at, slot):
-        to = goal_s[slot // 128, slot % 128]
-        placed[pl.ds(to, 1), :] = origin[pl.ds(at, 1), :]
-        placed[pl.ds(to + 1, 1), :] = origin[pl.ds(at + 1, 1), :]
+    for fetch in fetches:
+        fetch.wait()
+
+    def copy(row, slot):
+        kept[pl.ds(goal_s[slot // 128, slot % 128], 2, stride=8), :] = mixed[
+            pl.ds(16 * (row // 8) + row % 8, 2, stride=8), :
+        ]
 
     for s in range(N_COMP * SPREAD):
-        copy(spread_ref, PACKET * (s // SPREAD) + 2 * (s % SPREAD), s)
-    for s in range(NEAR_COMP):
-        copy(up_ref, 2 + 2 * s, 512 + s)
-    for s in range(NEAR_COMP):
-        copy(down_ref, 2 + 2 * s, 768 + s)
-    for s in range(NEAR_IO):
-        copy(next_ref, 2 + 2 * s, 1024 + s)
-    for s in range(NEAR_IO):
-        copy(prev_ref, 2 + 2 * s, 1280 + s)
-    for s in range(SPREAD):
-        copy(far_ref, 1 + 2 * s, 1536 + s)
-
-    copies = []
-    start = 0
-    for j, size in enumerate(SIZES):
-        left = placed[pl.ds(2 * start, size, stride=2), :]
-        right = placed[pl.ds(2 * start + 1, size, stride=2), :]
-        x = jnp.concatenate([left, right], axis=1)
-        x_high = x.astype(jnp.bfloat16)
-        x_low = (x - x_high.astype(jnp.float32)).astype(jnp.bfloat16)
-        total = jnp.dot(x_high, high_ref[...], preferred_element_type=jnp.float32)
-        total += jnp.dot(x_high, low_ref[...], preferred_element_type=jnp.float32)
-        total += jnp.dot(x_low, high_ref[...], preferred_element_type=jnp.float32)
-        result[start : start + size, :] = total
+        copy(N_COMP * (s % SPREAD) + s // SPREAD, s)
+    row = N_COMP * SPREAD
+    for base, count in ((512, NEAR_COMP), (768, NEAR_COMP), (1024, NEAR_IO), (1280, NEAR_IO), (1536, SPREAD)):
+        for s in range(count):
+            copy(row + s, base + s)
+        row += count
+    writes = []
+    for q in range(4):
         write = pltpu.make_async_copy(
-            result.at[pl.ds(start, size), :], out_ref.at[pl.ds(start, size), :], sems.at[2 + j]
+            kept.at[pl.ds(part * q, part), :], out_ref.at[pl.ds(part * q, part), :], sems.at[1 + q]
         )
         write.start()
-        copies.append(write)
-        start += size
-    for write in copies:
+        writes.append(write)
+    for write in writes:
         write.wait()
 
 
@@ -286,7 +320,6 @@
     f32 = jnp.float32
     whole = pl.BlockSpec(memory_space=VMEM)
     anywhere = pl.BlockSpec(memory_space=pl.ANY)
-    scalars = pl.BlockSpec(memory_space=SMEM)
     fields = (
         fields.reshape(COLUMNS // 8, 8, 2, 128).transpose(0, 2, 1, 3).reshape(2 * COLUMNS, 128)
     )
@@ -330,41 +363,49 @@
     after = shift(after, "io", 1)
     before = shift(before, "io", -1)
     far = shift(far, "io", 2)
-    placed, high, low = pl.pallas_call(
+    kept, high, low = pl.pallas_call(
         local_kernel,
         name="local",
         out_shape=[
-            pltpu.HBM((PLACED, 128), f32),
+            pltpu.HBM((COLUMNS, WIDTH), f32),
             VMEM((WIDTH, WIDTH), jnp.bfloat16),
             VMEM((WIDTH, WIDTH), jnp.bfloat16),
         ],
-        in_specs=[scalars, anywhere, whole],
-        out_specs=[whole] * 3,
-        scratch_shapes=[VMEM((2 * COLUMNS, 128), f32), pltpu.SemaphoreType.DMA((4,))],
+        in_specs=[anywhere, anywhere, whole],
+        out_specs=[anywhere, whole, whole],
+        scratch_shapes=[
+            VMEM((2 * COLUMNS, 128), f32),
+            VMEM((PLACED, 128), f32),
+            VMEM((COLUMNS, WIDTH), f32),
+            SMEM((BLOCKS, 128), jnp.int32),
+            pltpu.SemaphoreType.DMA((5 + COLUMNS // 512,)),
+        ],
         compiler_params=pltpu.CompilerParams(vmem_limit_bytes=40 * 2**20),
         cost_estimate=pl.CostEstimate(flops=4_000_000_000, bytes_accessed=6_000_000, transcendentals=0),
-    )(stay, fields, level_remap)
+    )(pltpu.with_memory_space_constraint(stay, pltpu.HBM), fields, level_remap)
+    kept = kept.reshape(COLUMNS // 8, 8, 2, 128).transpose(0, 2, 1, 3).reshape(2 * COLUMNS, 128)
     operands = [
         pltpu.with_memory_space_constraint(x, VMEM)
         for x in (spread, up, down, after, before, far, high, low)
     ]
-    operands.insert(6, pltpu.with_memory_space_constraint(placed, pltpu.HBM))
-    return pl.pallas_call(
+    operands.insert(6, pltpu.with_memory_space_constraint(kept, pltpu.HBM))
+    out = pl.pallas_call(
         final_kernel,
         name="final",
-        out_shape=jax.ShapeDtypeStruct((COLUMNS, WIDTH), f32),
+        out_shape=jax.ShapeDtypeStruct((2 * COLUMNS, 128), f32),
         in_specs=[whole] * 6 + [anywhere, whole, whole],
         out_specs=anywhere,
         scratch_shapes=[
             VMEM((PLACED, 128), f32),
             VMEM((16, 128), jnp.int32),
             SMEM((16, 128), jnp.int32),
-            VMEM((COLUMNS, WIDTH), f32),
-            pltpu.SemaphoreType.DMA((2 + len(SIZES),)),
+            VMEM((2 * RECEIVED, 128), f32),
+            pltpu.SemaphoreType.DMA((5,)),
         ],
         compiler_params=pltpu.CompilerParams(vmem_limit_bytes=40 * 2**20),
         cost_estimate=pl.CostEstimate(flops=1_000_000_000, bytes_accessed=8_000_000, transcendentals=0),
     )(*operands)
+    return out.reshape(COLUMNS // 8, 2, 8, 128).transpose(0, 2, 1, 3).reshape(COLUMNS, WIDTH)
 
 
 def solution(mesh):

time: 48.5 us -> 47.7 us (0.984)
  Pallas kernels: 16.2 us -> 14.1 us
  waiting for transfers between devices: 6.96 us -> 8.82 us
  local copies, waits for them, and re-layouts: 0.71 us -> 0.01 us
    ppermute x5, waiting for transfers between devices: 6.96 us -> 8.82 us  [shift(): lax.ppermute(value, axis, [(i, (i + by) % peers) for i in range(peers)])]
    pallas_call x1, Pallas kernels: 6.49 us -> 5.34 us  [per_device(): pl.pallas_call(local_kernel, name='local', out_shape=[pltpu.HBM((COLUMNS,...]
    unnamed x4 -> x2, local copies, waits for them, and re-layouts: 0.71 us -> 0.01 us
    pallas_call x1, Pallas kernels: 5.16 us -> 4.57 us  [per_device(): pl.pallas_call(final_kernel, name='final', out_shape=jax.ShapeDtypeStruct...]
  transfers between devices with their start and end apart: 6 -> 6, of which waited for: 2 -> 2; matrix products, arithmetic and copies ran while one was open for 0% -> 0% of each run, Pallas kernels for 13% -> 11%
where the time goes in v3:
time: 47.7 us; the launch traced here: 47.4 us
  starting transfers between devices  24.4 us (51%)
  Pallas kernels  14.1 us (30%)
  waiting for transfers between devices  8.82 us (18%)
    all_to_all x1, starting transfers between devices, per_device(): lax.all_to_all(spread.reshape(N_COMP, 1, PACKET * 128), 'comp', split_axi...  13.5 us
    ppermute x5, starting transfers between devices, shift(): lax.ppermute(value, axis, [(i, (i + by) % peers) for i in range(peers)])  10.9 us
    ppermute x5, waiting for transfers between devices, shift(): lax.ppermute(value, axis, [(i, (i + by) % peers) for i in range(peers)])  8.82 us
    pallas_call x1, Pallas kernels, per_device(): pl.pallas_call(local_kernel, name='local', out_shape=[pltpu.HBM((COLUMNS,...  5.34 us
    pallas_call x1, Pallas kernels, per_device(): pl.pallas_call(final_kernel, name='final', out_shape=jax.ShapeDtypeStruct...  4.57 us
    pallas_call x1, Pallas kernels, per_device(): pl.pallas_call(pack_kernel, name='pack', out_shape=[pltpu.HBM((N_COMP * P...  4.22 us
  transfers between devices with their start and end apart: 6, of which 2 were waited for; matrix products, arithmetic and copies ran while one was open for 0% of the time, Pallas kernels for 11%

profile of v3, /device:TPU:1, one launch (start us, length us, event | category | flops | bytes accessed | tf_op | source)
XLA Modules:
  0.0 47.4 jit_solution(13204257487944209987)
XLA Ops:
  0.0 0.0 copy-start
  0.0 4.2 %pack.1 = (f32[1088,128]{1,0:T(8,128)}, f32[392,128]{1,0:T(8,128)S(1)}, f32[392,128]{1,0:T(8,128)S(1)}, f32[408,128]{1,0:T(8,128)S(1)}, f32[408,128]{1,0:T(8,128...) custom-call(s32[24,128]{1,0:T(8,128)} %offsets_ref.1, f32[6144,128]{1,0:T(8,128)} %bitcast.18), custom_call_target="tpu_custom_call" | custom-call | flops 20000000 | bytes 5000000 | tf_op jit(solution)/shard_map/pack/pallas_call | solution.py:328
  4.2 13.5 %all-to-all-start = ((f32[64,1,2176]{2,1,0:T(1,128)}), f32[64,1,2176]{2,1,0:T(1,128)S(1)}, u32[]{:S(2)}, u32[]{:S(2)}) async-start(f32[64,1,2176]{2,1,0:T(1,128)} %bitcast.21), calls=%async_computation | async-start | bytes 1114112 | tf_op jit(solution)/shard_map/all_to_all | solution.py:358
  17.7 2.7 %collective-permute-start.4 = (f32[24,128]{1,0:T(8,128)S(1)}, f32[24,128]{1,0:T(8,128)S(1)}, u32[]{:S(2)}, u32[]{:S(2)}) collective-permute-start(f32[24,128]{1,0:T(8,128)S(1)} %get-tuple-element.20), channel_id=1, source_target_pairs={{0,128},{64,192},{128,0},{192,64},{1,129},{65,193},{129,1},{193,65... | collective-permute-start | bytes 36872 | tf_op jit(solution)/shard_map/ppermute | solution.py:316
  20.4 1.0 %collective-permute-start = (f32[392,128]{1,0:T(8,128)S(1)}, f32[392,128]{1,0:T(8,128)S(1)}, u32[]{:S(2)}, u32[]{:S(2)}) collective-permute-start(f32[392,128]{1,0:T(8,128)S(1)} %get-tuple-element.16), channel_id=1, source_target_pairs={{0,1},{1,2},{2,3},{3,4},{4,5},{5,6},{6,7},{7,8},{8,9},{9,10},{10,1... | collective-permute-start | bytes 602120 | tf_op jit(solution)/shard_map/ppermute | solution.py:316
  21.5 4.7 %collective-permute-start.1 = (f32[392,128]{1,0:T(8,128)S(1)}, f32[392,128]{1,0:T(8,128)S(1)}, u32[]{:S(2)}, u32[]{:S(2)}) collective-permute-start(f32[392,128]{1,0:T(8,128)S(1)} %get-tuple-element.17), channel_id=1, source_target_pairs={{0,63},{1,0},{2,1},{3,2},{4,3},{5,4},{6,5},{7,6},{8,7},{9,8},{10,9... | collective-permute-start | bytes 602120 | tf_op jit(solution)/shard_map/ppermute | solution.py:316
  26.1 2.5 %collective-permute-start.2 = (f32[408,128]{1,0:T(8,128)S(1)}, f32[408,128]{1,0:T(8,128)S(1)}, u32[]{:S(2)}, u32[]{:S(2)}) collective-permute-start(f32[408,128]{1,0:T(8,128)S(1)} %get-tuple-element.18), channel_id=1, source_target_pairs={{0,64},{64,128},{128,192},{192,0},{1,65},{65,129},{129,193},{193,1... | collective-permute-start | bytes 626696 | tf_op jit(solution)/shard_map/ppermute | solution.py:316
  28.6 0.0 collective-permute-start.3
  28.6 0.0 copy-done
  28.6 5.3 %local.1 = (f32[3072,256]{1,0:T(8,128)}, bf16[256,256]{1,0:T(8,128)(2,1)S(1)}, bf16[256,256]{1,0:T(8,128)(2,1)S(1)}) custom-call(s32[24,128]{1,0:T(8,128)} %get-tuple-element.21.stay_in, f32[6144,128]{1,0:T(8,128)} %bitcast.19, f32[4,64,64]{2,1,0:T(8,128)S(1)} %copy-done), custom_call_target="tpu_custom_call" | custom-call | flops 4000000000 | bytes 6000000 | tf_op jit(solution)/shard_map/local/pallas_call | solution.py:366
  34.0 0.0 collective-permute-done.4.far_ref
  34.0 5.6 %collective-permute-done.up_ref = f32[392,128]{1,0:T(8,128)S(1)} collective-permute-done((f32[392,128]{1,0:T(8,128)S(1)}, f32[392,128]{1,0:T(8,128)S(1)}, u32[]{:S(2)}, u32[]{:S(2)}) %collective-permute-start) | collective-permute-done | bytes 200736 | tf_op jit(solution)/shard_map/ppermute | solution.py:316
  39.6 0.0 collective-permute-done.1.down_ref
  39.6 0.0 collective-permute-done.2.next_ref
  39.6 3.2 %collective-permute-done.3.prev_ref = f32[408,128]{1,0:T(8,128)S(1)} collective-permute-done((f32[408,128]{1,0:T(8,128)S(1)}, f32[408,128]{1,0:T(8,128)S(1)}, u32[]{:S(2)}, u32[]{:S(2)}) %collective-permute-start.3) | collective-permute-done | bytes 208928 | tf_op jit(solution)/shard_map/ppermute | solution.py:316
  42.8 0.0 all-to-all-done
  42.8 4.6 %final.1 = f32[6144,128]{1,0:T(8,128)} custom-call(f32[1088,128]{1,0:T(8,128)S(1)} %bitcast.17, f32[392,128]{1,0:T(8,128)S(1)} %collective-permute-done.up_ref, f32[392,128]{1,0:T(8,128)S(1)} %collective-permute-done.1.down_ref, f32[408,128]{1,0:T(8,128)S(1)} %collective-permute-done.2.next_ref, f32[408,128]{1,0:T(8,128)S(1)} %collective-permute-done.3.prev_ref, ...), custom_call_target="tpu_custom_call" | custom-call | flops 1000000000 | bytes 8000000 | tf_op jit(solution)/shard_map/final/pallas_call | solution.py:392
Async XLA Ops:
  0.0 28.6 %copy-start = (f32[4,64,64]{2,1,0:T(8,128)S(1)}, f32[4,64,64]{2,1,0:T(8,128)}, u32[]{:S(2)}) copy-start(f32[4,64,64]{2,1,0:T(8,128)} %remap_ref.1) | copy-start | bytes 196612
  4.2 38.6 %all-to-all-start = ((f32[64,1,2176]{2,1,0:T(1,128)}), f32[64,1,2176]{2,1,0:T(1,128)S(1)}, u32[]{:S(2)}, u32[]{:S(2)}) async-start(f32[64,1,2176]{2,1,0:T(1,128)} %bitcast.21), calls=%async_computation | async-start | bytes 1114112 | tf_op jit(solution)/shard_map/all_to_all | solution.py:358
  17.7 16.2 %collective-permute-start.4 = (f32[24,128]{1,0:T(8,128)S(1)}, f32[24,128]{1,0:T(8,128)S(1)}, u32[]{:S(2)}, u32[]{:S(2)}) collective-permute-start(f32[24,128]{1,0:T(8,128)S(1)} %get-tuple-element.20), channel_id=1, source_target_pairs={{0,128},{64,192},{128,0},{192,64},{1,129},{65,193},{129,1},{193,65... | collective-permute-start | bytes 36872 | tf_op jit(solution)/shard_map/ppermute | solution.py:316
  20.4 19.1 %collective-permute-start = (f32[392,128]{1,0:T(8,128)S(1)}, f32[392,128]{1,0:T(8,128)S(1)}, u32[]{:S(2)}, u32[]{:S(2)}) collective-permute-start(f32[392,128]{1,0:T(8,128)S(1)} %get-tuple-element.16), channel_id=1, source_target_pairs={{0,1},{1,2},{2,3},{3,4},{4,5},{5,6},{6,7},{7,8},{8,9},{9,10},{10,1... | collective-permute-start | bytes 602120 | tf_op jit(solution)/shard_map/ppermute | solution.py:316
  21.5 18.1 %collective-permute-start.1 = (f32[392,128]{1,0:T(8,128)S(1)}, f32[392,128]{1,0:T(8,128)S(1)}, u32[]{:S(2)}, u32[]{:S(2)}) collective-permute-start(f32[392,128]{1,0:T(8,128)S(1)} %get-tuple-element.17), channel_id=1, source_target_pairs={{0,63},{1,0},{2,1},{3,2},{4,3},{5,4},{6,5},{7,6},{8,7},{9,8},{10,9... | collective-permute-start | bytes 602120 | tf_op jit(solution)/shard_map/ppermute | solution.py:316
  26.1 13.4 %collective-permute-start.2 = (f32[408,128]{1,0:T(8,128)S(1)}, f32[408,128]{1,0:T(8,128)S(1)}, u32[]{:S(2)}, u32[]{:S(2)}) collective-permute-start(f32[408,128]{1,0:T(8,128)S(1)} %get-tuple-element.18), channel_id=1, source_target_pairs={{0,64},{64,128},{128,192},{192,0},{1,65},{65,129},{129,193},{193,1... | collective-permute-start | bytes 626696 | tf_op jit(solution)/shard_map/ppermute | solution.py:316
  28.6 14.2 %collective-permute-start.3 = (f32[408,128]{1,0:T(8,128)S(1)}, f32[408,128]{1,0:T(8,128)S(1)}, u32[]{:S(2)}, u32[]{:S(2)}) collective-permute-start(f32[408,128]{1,0:T(8,128)S(1)} %get-tuple-element.19), channel_id=1, source_target_pairs={{0,192},{64,0},{128,64},{192,128},{1,193},{65,1},{129,65},{193,129... | collective-permute-start | bytes 626696 | tf_op jit(solution)/shard_map/ppermute | solution.py:316
